TPU v7x, 512 devices: a whole 4x8x8 slice. The times are simulated.
512 devices in a mesh: dom: 32 (over z, x), snap: 16 (over y, core).
Axes of the slice: x: 4, y: 8, z: 8, core: 2. Of those that a mesh axis runs over, the one named last changes fastest.
Arguments:
- feat: bfloat16 [16, 4096, 512], P('snap', 'dom'), may hold values from -6 to 6
- w_struct: bfloat16 [512, 1536], replicated, may hold values from -0.25 to 0.25
- w_temp: bfloat16 [512, 1536], replicated, may hold values from -0.25 to 0.25
- pos_embed: bfloat16 [16, 512], replicated, may hold values from -3 to 3
- rel_bias: float32 [4, 8], replicated, may hold values from -1.5 to 1.5
- nbr: int32 [16, 4096, 8], P('snap', 'dom'), may hold values from 0 to 383
- rel_type: int32 [16, 4096, 8], P('snap', 'dom'), may hold values from 0 to 3
- send_idx: int32 [16, 32, 32, 8], P('snap', 'dom'), may hold values from 0 to 127
- active: int32 [16, 4096], P(None, ('dom', 'snap')), may hold values 0 or 1
- cotangent: bfloat16 [16, 4096, 512], P(None, ('dom', 'snap')), may hold values from -6 to 6
Outputs:
- grad_feat: bfloat16 [16, 4096, 512], P('snap', 'dom')
- grad_wtemp: float32 [512, 1536], P('snap')
Inputs may be any that keep to these rules, and one draw needn't show every extreme that they name: `nbr`: rows of the partition's key table: its 128 own entities first, then 8 halo rows from each partition in order.
All inputs are finite; a program needn't handle non-finite values. No bound on the sum of `active` on one device may be relied on, other than what follows from the above.
Results may differ from a plain program's by a relative error of at most 0.024.
Values may be sent and summed in bfloat16 or wider, within the bound.
A program may use at most 64 MiB of HBM per device.

v0:
```python
import jax
import jax.numpy as jnp
from jax import lax
from jax.sharding import PartitionSpec as P

HEADS = 8


def edge_scores(rel_ids, rel_bias):
    onehot = (rel_ids[..., None] == jnp.arange(rel_bias.shape[0], dtype=jnp.int32)).astype(
        jnp.float32
    )
    return jnp.einsum("rek,kh->reh", onehot, rel_bias, precision=lax.Precision.HIGHEST)


def struct_core(query, key_tab, val_tab, links, edge_add):
    row_count, width = query.shape
    slots = links.shape[1]
    head_dim = width // HEADS
    keys_g = key_tab[links].reshape(row_count, slots, HEADS, head_dim)
    vals_g = val_tab[links].reshape(row_count, slots, HEADS, head_dim)
    query_h = query.reshape(row_count, HEADS, head_dim)
    scores = jnp.einsum("rhc,rehc->reh", query_h, keys_g) * head_dim ** (-0.5) + edge_add
    weights = jax.nn.softmax(scores, axis=1)
    rounded = lax.optimization_barrier(weights.astype(jnp.bfloat16)).astype(jnp.float32)
    return jnp.einsum("reh,rehc->rhc", rounded, vals_g).reshape(row_count, width)


def temp_allowed(active_blk):
    snaps = active_blk.shape[0]
    later = jnp.arange(snaps, dtype=jnp.int32)[:, None]
    earlier = jnp.arange(snaps, dtype=jnp.int32)[None, :]
    causal = (earlier <= later)[..., None]
    itself = (earlier == later)[..., None]
    return causal & (itself | (active_blk[None, :, :] == 1))


def temp_core(t_query, t_key, t_value, allowed):
    snaps, count, width = t_query.shape
    head_dim = width // HEADS
    query_h = t_query.reshape(snaps, count, HEADS, head_dim)
    key_h = t_key.reshape(snaps, count, HEADS, head_dim)
    value_h = t_value.reshape(snaps, count, HEADS, head_dim)
    scores = jnp.einsum("tmhc,umhc->tumh", query_h, key_h) * head_dim ** (-0.5)
    scores = jnp.where(allowed[..., None], scores, -1e30)
    weights = jax.nn.softmax(scores, axis=1)
    rounded = lax.optimization_barrier(weights.astype(jnp.bfloat16)).astype(jnp.float32)
    return jnp.einsum("tumh,umhc->tmhc", rounded, value_h).reshape(snaps, count, width)


def per_device(
    feat, w_struct, w_temp, pos_embed, rel_bias, nbr, rel_type, send_idx, active, cotangent
):
    x_rows = feat[0]
    local_count, width = x_rows.shape
    dom_count = lax.axis_size("dom")
    route = send_idx[0, 0]
    halo_per = route.shape[1]
    route_flat = route.reshape(-1)
    projected = jnp.dot(x_rows, w_struct, preferred_element_type=jnp.float32).astype(jnp.bfloat16)
    pair_cols = projected[:, width:]
    tiles = pair_cols[route_flat].reshape(dom_count, halo_per, 2 * width)
    arrived = lax.all_to_all(tiles, "dom", split_axis=0, concat_axis=0, tiled=True).reshape(
        -1, 2 * width
    )
    query_f = projected[:, :width].astype(jnp.float32)
    table = jnp.concatenate([pair_cols, arrived], axis=0).astype(jnp.float32)
    edge_add = edge_scores(rel_type[0], rel_bias)
    links = nbr[0]
    summed = struct_core(query_f, table[:, :width], table[:, width:], links, edge_add)
    hidden = (x_rows.astype(jnp.float32) + jax.nn.elu(summed)).astype(jnp.bfloat16)
    by_entity = lax.all_to_all(hidden[None], "snap", split_axis=1, concat_axis=0, tiled=True)
    snaps = by_entity.shape[0]
    z_in = (by_entity.astype(jnp.float32) + pos_embed.astype(jnp.float32)[:, None, :]).astype(
        jnp.bfloat16
    )
    z_flat = z_in.reshape(-1, width)
    t_proj = jnp.dot(z_flat, w_temp, preferred_element_type=jnp.float32).astype(jnp.bfloat16)
    t_proj = t_proj.reshape(snaps, -1, 3 * width).astype(jnp.float32)
    allowed = temp_allowed(active)
    cot_f = cotangent.astype(jnp.float32)
    _, pull = jax.vjp(
        lambda a_in, b_in, c_in: temp_core(a_in, b_in, c_in, allowed),
        t_proj[..., :width],
        t_proj[..., width : 2 * width],
        t_proj[..., 2 * width :],
    )
    grads_t = pull(cot_f)
    dt_proj = jnp.concatenate(grads_t, axis=-1).astype(jnp.bfloat16).reshape(-1, 3 * width)
    terms = lax.dot_general(
        z_flat, dt_proj, (((0,), (0,)), ((), ())), preferred_element_type=jnp.float32
    )
    share = lax.psum_scatter(terms.astype(jnp.bfloat16), "snap", scatter_dimension=0, tiled=True)
    grad_wtemp = lax.psum(share, "dom").astype(jnp.float32)
    d_z = cot_f + jnp.dot(dt_proj, w_temp.T, preferred_element_type=jnp.float32).reshape(
        snaps, -1, width
    )
    returned = lax.all_to_all(
        d_z.astype(jnp.bfloat16), "snap", split_axis=0, concat_axis=1, tiled=True
    )[0]
    dh_f = returned.astype(jnp.float32)
    d_agg = dh_f * jnp.where(summed > 0, 1.0, jnp.exp(summed))
    _, pull_s = jax.vjp(
        lambda a_in, b_in, c_in: struct_core(a_in, b_in, c_in, links, edge_add),
        query_f,
        table[:, :width],
        table[:, width:],
    )
    d_query, d_key, d_val = pull_s(d_agg)
    halo_back = jnp.concatenate([d_key[local_count:], d_val[local_count:]], axis=-1)
    halo_back = halo_back.reshape(dom_count, halo_per, 2 * width)
    came_back = (
        lax.all_to_all(
            halo_back.astype(jnp.bfloat16), "dom", split_axis=0, concat_axis=0, tiled=True
        )
        .astype(halo_back.dtype)
        .reshape(-1, 2 * width)
    )
    owned = jnp.concatenate([d_key[:local_count], d_val[:local_count]], axis=-1)
    owned = owned.at[route_flat].add(came_back)
    d_proj = jnp.concatenate([d_query, owned], axis=-1).astype(jnp.bfloat16)
    grad_rows = (dh_f + jnp.dot(d_proj, w_struct.T, preferred_element_type=jnp.float32)).astype(
        jnp.bfloat16
    )
    return (grad_rows[None], grad_wtemp)


def solution(mesh):
    return jax.shard_map(
        per_device,
        mesh=mesh,
        in_specs=(
            P("snap", "dom", None),
            P(),
            P(),
            P(),
            P(),
            P("snap", "dom", None),
            P("snap", "dom", None),
            P("snap", "dom", None, None),
            P(None, ("dom", "snap")),
            P(None, ("dom", "snap"), None),
        ),
        out_specs=(P("snap", "dom", None), P("snap", None)),
        check_vma=False,
    )
```

profile of v0, /device:TPU:24, one launch (start us, length us, event | category | flops | bytes accessed | tf_op | source)
XLA Modules:
  0.0 353.6 jit_solution(8830739789273474780)
XLA Ops:
  12.3 13.3 %all-to-all-start = ((bf16[32,8,1024]{2,1,0:T(8,128)(2,1)}), bf16[32,8,1024]{2,1,0:T(8,128)(2,1)S(1)}, u32[]{:S(2)}, u32[]{:S(2)}) async-start(bf16[32,8,1024]{2,1,0:T(8,128)(2,1)} %bitcast.7), calls=%async_computation | async-start | bytes 1048576 | tf_op jit(solution)/shard_map/all_to_all | solution.py:63
  27.3 16.1 %all-to-all-done = bf16[32,8,1024]{2,1,0:T(8,128)(2,1)S(1)} async-done(((bf16[32,8,1024]{2,1,0:T(8,128)(2,1)}), bf16[32,8,1024]{2,1,0:T(8,128)(2,1)S(1)}, u32[]{:S(2)}, u32[]{:S(2)}) %all-to-all-start) | async-done | bytes 524320 | tf_op jit(solution)/shard_map/all_to_all | solution.py:63
  45.2 5.1 %gather_fusion.1 = bf16[1024,512]{1,0:T(8,128)(2,1)} fusion(bf16[384,512]{1,0:T(8,128)(2,1)S(1)} %get-tuple-element.3, s32[1024]{0:T(1024)S(1)} %get-tuple-element.20), kind=kCustom, calls=%fused_computation.1 | custom fusion | bytes 2101248 | tf_op jit(solution)/shard_map/gather | solution.py:20
  50.3 3.9 %reshape.244 = bf16[128,8,8,64]{3,2,1,0:T(8,128)(2,1)} reshape(bf16[1024,512]{1,0:T(8,128)(2,1)} %gather_fusion.1) | data formatting | bytes 2097152 | tf_op jit(solution)/shard_map/reshape | solution.py:20
  54.2 3.6 %multiply_reduce_fusion.3 = f32[128,8,8]{1,2,0:T(8,128)} fusion(f32[128,8,64]{2,1,0:T(8,128)S(1)} %copy.120, bf16[128,8,8,64]{3,2,1,0:T(8,128)(2,1)} %reshape.244), kind=kLoop, calls=%fused_computation.10 | loop fusion | flops 1564672 | bytes 1343488
  60.3 5.1 %gather_fusion.2 = bf16[1024,512]{1,0:T(8,128)(2,1)} fusion(bf16[384,512]{1,0:T(8,128)(2,1)S(1)} %get-tuple-element.2, s32[1024]{0:T(1024)S(1)} %get-tuple-element.20), kind=kCustom, calls=%fused_computation.2 | custom fusion | bytes 2101248 | tf_op jit(solution)/shard_map/gather | solution.py:21
  65.4 4.0 %reshape.246 = bf16[128,8,8,64]{3,2,1,0:T(8,128)(2,1)} reshape(bf16[1024,512]{1,0:T(8,128)(2,1)} %gather_fusion.2) | data formatting | bytes 2097152 | tf_op jit(solution)/shard_map/reshape | solution.py:21
  69.3 2.6 multiply_reduce_fusion.2
  76.0 7.4 %all-to-all-start.1 = ((bf16[16,2,2048]{2,1,0:T(2,128)(2,1)}), bf16[16,2,2048]{2,1,0:T(2,128)(2,1)S(1)}, u32[]{:S(2)}, u32[]{:S(2)}) async-start(bf16[16,2,2048]{2,1,0:T(2,128)(2,1)} %reshape.337), calls=%async_computation.1 | async-start | bytes 262144 | tf_op jit(solution)/shard_map/all_to_all | solution.py:72
  84.0 5.7 %all-to-all-done.1 = bf16[16,2,2048]{2,1,0:T(2,128)(2,1)S(1)} async-done(((bf16[16,2,2048]{2,1,0:T(2,128)(2,1)}), bf16[16,2,2048]{2,1,0:T(2,128)(2,1)S(1)}, u32[]{:S(2)}, u32[]{:S(2)}) %all-to-all-start.1) | async-done | bytes 131104 | tf_op jit(solution)/shard_map/all_to_all | solution.py:72
  99.6 2.3 fusion.10
  112.4 2.9 fusion.1
  116.6 5.8 %all-to-all-start.2 = ((bf16[16,8,512]{2,1,0:T(8,128)(2,1)}), bf16[16,8,512]{2,1,0:T(8,128)(2,1)S(1)}, u32[]{:S(2)}, u32[]{:S(2)}) async-start(bf16[16,8,512]{2,1,0:T(8,128)(2,1)} %fusion.17), calls=%async_computation.2 | async-start | bytes 262144 | tf_op jit(solution)/shard_map/all_to_all | solution.py:98
  123.4 5.7 %all-to-all-done.2 = bf16[16,8,512]{2,1,0:T(8,128)(2,1)S(1)} async-done(((bf16[16,8,512]{2,1,0:T(8,128)(2,1)}), bf16[16,8,512]{2,1,0:T(8,128)(2,1)S(1)}, u32[]{:S(2)}, u32[]{:S(2)}) %all-to-all-start.2) | async-done | bytes 131104 | tf_op jit(solution)/shard_map/all_to_all | solution.py:98
  129.8 5.6 %multiply_reduce_fusion.1 = (bf16[128,8,8]{1,2,0:T(8,128)(2,1)S(1)}, f32[128,8,8,64]{3,2,1,0:T(8,128)}) fusion(f32[128,8,64]{2,1,0:T(8,128)S(1)} %copy.122, bf16[128,8,8,64]{3,2,1,0:T(8,128)(2,1)} %reshape.246, f32[128,8,8]{1,2,0:T(8,128)} %copy.90), kind=kLoop, calls=%fused_computation.8 | loop fusion | flops 2088960 | bytes 3457024
  135.4 4.8 %reshape.300 = f32[1024,512]{1,0:T(8,128)} reshape(f32[128,8,8,64]{3,2,1,0:T(8,128)} %get-tuple-element.7) | data formatting | bytes 4194304 | tf_op jit(solution)/shard_map/transpose(jvp())/reshape | solution.py:21
  140.7 5.6 %multiply_reduce_fusion = (bf16[128,8,64]{2,1,0:T(8,128)(2,1)}, f32[128,8,8,64]{3,2,1,0:T(8,128)}) fusion(f32[128,8,8]{1,2,0:T(8,128)S(1)} %copy.123, bf16[128,8,8,64]{3,2,1,0:T(8,128)(2,1)} %reshape.244, f32[128,8,64]{2,1,0:T(8,128)S(1)} %copy.120), kind=kLoop, calls=%fused_computation.7 | loop fusion | flops 2031616 | bytes 3571712
  146.3 4.8 %reshape.292 = f32[1024,512]{1,0:T(8,128)} reshape(f32[128,8,8,64]{3,2,1,0:T(8,128)} %get-tuple-element.5) | data formatting | bytes 4194304 | tf_op jit(solution)/shard_map/transpose(jvp())/reshape | solution.py:20
  151.1 7.5 %scatter_custom_fusion.1 = f32[384,512]{1,0:T(8,128)S(1)} fusion(s32[1024]{0:T(1024)S(1)} %reshape.274, f32[1024,512]{1,0:T(8,128)} %reshape.300, f32[]{:T(128)} %constant.15.clone.1), kind=kCustom, calls=%fused_computation.65 | custom fusion | flops 524288 | bytes 786944 | tf_op jit(solution)/shard_map/transpose(jvp())/scatter-add | solution.py:21
  158.6 7.5 %scatter_custom_fusion = f32[384,512]{1,0:T(8,128)S(1)} fusion(s32[1024]{0:T(1024)S(1)} %reshape.274, f32[1024,512]{1,0:T(8,128)} %reshape.292, f32[]{:T(128)} %constant.15.clone.1), kind=kCustom, calls=%fused_computation.67 | custom fusion | flops 524288 | bytes 786944 | tf_op jit(solution)/shard_map/transpose(jvp())/scatter-add | solution.py:20
  167.1 4.6 %all-to-all-start.3 = ((bf16[32,8,1024]{2,1,0:T(8,128)(2,1)}), bf16[32,8,1024]{2,1,0:T(8,128)(2,1)}, u32[]{:S(2)}, u32[]{:S(2)}) async-start(bf16[32,8,1024]{2,1,0:T(8,128)(2,1)} %maximum_bitcast_fusion), calls=%async_computation.3 | async-start | bytes 1048576 | tf_op jit(solution)/shard_map/all_to_all | solution.py:113
  179.1 11.1 %all-to-all-done.3 = bf16[32,8,1024]{2,1,0:T(8,128)(2,1)} async-done(((bf16[32,8,1024]{2,1,0:T(8,128)(2,1)}), bf16[32,8,1024]{2,1,0:T(8,128)(2,1)}, u32[]{:S(2)}, u32[]{:S(2)}) %all-to-all-start.3) | async-done | bytes 524320 | tf_op jit(solution)/shard_map/all_to_all | solution.py:113
  190.2 5.0 %scatter_custom_fusion.2 = f32[128,1024]{1,0:T(8,128)} fusion(f32[128,1024]{1,0:T(8,128)} %pad_maximum_fusion, s32[256]{0:T(256)S(1)} %bitcast.139, bf16[32,8,1024]{2,1,0:T(8,128)(2,1)} %all-to-all-done.3), kind=kCustom, calls=%fused_computation.39 | custom fusion | flops 524288 | bytes 1048576 | tf_op jit(solution)/shard_map/scatter-add | solution.py:120
  198.5 146.7 %all-reduce.2.cloned.1.call-done = bf16[32,1536]{1,0:T(8,128)(2,1)} async-done(((bf16[32,1536]{1,0:T(8,128)(2,1)}), bf16[32,1536]{1,0:T(8,128)(2,1)}) %all-reduce.2.cloned.1.call-update) | async-done | bytes 98320 | tf_op jit(solution)/shard_map/psum | solution.py:94
  (124 shorter events, 52.7 us)
Async XLA Ops:
  7.2 82.7 %copy-start = (bf16[512,1536]{1,0:T(8,128)(2,1)S(1)}, bf16[512,1536]{1,0:T(8,128)(2,1)}, u32[]{:S(2)}) copy-start(bf16[512,1536]{1,0:T(8,128)(2,1)} %param.12) | copy-start | bytes 4718596
  7.2 2.9 copy-start.15
  10.3 15.3 %copy-start.12 = (bf16[1,128,512]{2,1,0:T(8,128)(2,1)S(1)}, bf16[1,128,512]{2,1,0:T(8,128)(2,1)}, u32[]{:S(2)}) copy-start(bf16[1,128,512]{2,1,0:T(8,128)(2,1)} %param.10) | copy-start | bytes 393220
  12.3 14.4 %copy-start.17 = (s32[16,8]{0,1:T(8,128)S(1)}, s32[16,8]{0,1:T(8,128)}, u32[]{:S(2)}) copy-start(s32[16,8]{0,1:T(8,128)} %param.18) | copy-start | bytes 1540
  12.3 31.1 %all-to-all-start = ((bf16[32,8,1024]{2,1,0:T(8,128)(2,1)}), bf16[32,8,1024]{2,1,0:T(8,128)(2,1)S(1)}, u32[]{:S(2)}, u32[]{:S(2)}) async-start(bf16[32,8,1024]{2,1,0:T(8,128)(2,1)} %bitcast.7), calls=%async_computation | async-start | bytes 1048576 | tf_op jit(solution)/shard_map/all_to_all | solution.py:63
  54.2 4.8 %copy-start.16 = (s32[1,128,8]{1,2,0:T(8,128)S(1)}, s32[1,128,8]{1,2,0:T(8,128)}, u32[]{:S(2)}) copy-start(s32[1,128,8]{1,2,0:T(8,128)} %param.16) | copy-start | bytes 12292
  54.2 4.8 %copy-start.19 = (f32[4,8]{1,0:T(4,128)S(1)}, f32[4,8]{1,0:T(4,128)}, u32[]{:S(2)}) copy-start(f32[4,8]{1,0:T(4,128)} %param.14) | copy-start | bytes 388
  65.3 4.0 %copy-start.4 = (f32[128,8,8]{1,2,0:T(8,128)S(1)}, f32[128,8,8]{1,2,0:T(8,128)}, u32[]{:S(2)}) copy-start(f32[128,8,8]{1,2,0:T(8,128)} %copy.121) | copy-start | bytes 98308
  71.9 11.7 %copy-start.14 = (bf16[16,512]{1,0:T(8,128)(2,1)S(1)}, bf16[16,512]{1,0:T(8,128)(2,1)}, u32[]{:S(2)}) copy-start(bf16[16,512]{1,0:T(8,128)(2,1)} %param.13) | copy-start | bytes 49156
  71.9 11.7 %copy-start.10 = (bf16[16,8,512]{2,1,0:T(8,128)(2,1)S(1)}, bf16[16,8,512]{2,1,0:T(8,128)(2,1)}, u32[]{:S(2)}) copy-start(bf16[16,8,512]{2,1,0:T(8,128)(2,1)} %param.19) | copy-start | bytes 393220
  71.9 11.9 %copy-start.18 = (pred[16,8]{0,1:T(8,128)(4,1)S(1)}, pred[16,8]{0,1:T(8,128)(4,1)}, u32[]{:S(2)}) copy-start(pred[16,8]{0,1:T(8,128)(4,1)} %broadcast_compare_fusion) | copy-start | bytes 388
  76.0 13.6 %all-to-all-start.1 = ((bf16[16,2,2048]{2,1,0:T(2,128)(2,1)}), bf16[16,2,2048]{2,1,0:T(2,128)(2,1)S(1)}, u32[]{:S(2)}, u32[]{:S(2)}) async-start(bf16[16,2,2048]{2,1,0:T(2,128)(2,1)} %reshape.337), calls=%async_computation.1 | async-start | bytes 262144 | tf_op jit(solution)/shard_map/all_to_all | solution.py:72
  83.4 112.8 %reduce-scatter.2.cloned.1.call-start = ((), (), s32[]{:S(2)}) async-start(), calls=%async_computation.5 | async-start | bytes 1671168 | tf_op jit(solution)/shard_map/reduce_scatter | solution.py:93
  84.0 11.3 %copy-start.13 = (pred[16,16,8]{0,1,2:T(8,128)(4,1)}, pred[16,16,8]{0,1,2:T(8,128)(4,1)S(1)}, u32[]{:S(2)}) copy-start(pred[16,16,8]{0,1,2:T(8,128)(4,1)S(1)} %or_and_fusion) | copy-start | bytes 6148
  92.1 6.7 %copy-start.6 = (bf16[16,8,8,64]{3,2,1,0:T(8,128)(2,1)}, bf16[16,8,8,64]{3,2,1,0:T(8,128)(2,1)S(1)}, u32[]{:S(2)}) copy-start(bf16[16,8,8,64]{3,2,1,0:T(8,128)(2,1)S(1)} %reshape.251) | copy-start | bytes 393220
  95.3 3.5 copy-start.5
  104.1 8.2 %copy-start.9 = (bf16[128,1,512]{2,1,0:T(2,128)(2,1)S(1)}, bf16[128,1,512]{2,1,0:T(2,128)(2,1)}, u32[]{:S(2)}) copy-start(bf16[128,1,512]{2,1,0:T(2,128)(2,1)} %copy-done.8) | copy-start | bytes 393220
  112.4 2.9 copy-start.7
  112.4 3.0 copy-start.11
  116.6 12.5 %all-to-all-start.2 = ((bf16[16,8,512]{2,1,0:T(8,128)(2,1)}), bf16[16,8,512]{2,1,0:T(8,128)(2,1)S(1)}, u32[]{:S(2)}, u32[]{:S(2)}) async-start(bf16[16,8,512]{2,1,0:T(8,128)(2,1)} %fusion.17), calls=%async_computation.2 | async-start | bytes 262144 | tf_op jit(solution)/shard_map/all_to_all | solution.py:98
  166.0 6.0 %copy-start.2 = (f32[384,512]{1,0:T(8,128)}, f32[384,512]{1,0:T(8,128)S(1)}, u32[]{:S(2)}) copy-start(f32[384,512]{1,0:T(8,128)S(1)} %scatter_custom_fusion) | copy-start | bytes 2359300
  167.1 23.0 %all-to-all-start.3 = ((bf16[32,8,1024]{2,1,0:T(8,128)(2,1)}), bf16[32,8,1024]{2,1,0:T(8,128)(2,1)}, u32[]{:S(2)}, u32[]{:S(2)}) async-start(bf16[32,8,1024]{2,1,0:T(8,128)(2,1)} %maximum_bitcast_fusion), calls=%async_computation.3 | async-start | bytes 1048576 | tf_op jit(solution)/shard_map/all_to_all | solution.py:113
  171.7 173.5 %all-reduce.2.cloned.1.call-start = ((), (), s32[]{:S(2)}) async-start(), calls=%async_computation.6 | async-start | bytes 196608 | tf_op jit(solution)/shard_map/psum | solution.py:94
  172.1 24.2 %copy-start.1 = (bf16[512,1536]{1,0:T(8,128)(2,1)S(1)}, bf16[512,1536]{1,0:T(8,128)(2,1)}, u32[]{:S(2)}) copy-start(bf16[512,1536]{1,0:T(8,128)(2,1)} %param.11) | copy-start | bytes 4718596
  (2 other events, 1.9 us)
Sparse Core Ops, SparseCore 0:
  115.4 54.3 reduce-scatter.1
  196.4 148.7 all-reduce.1
where the time goes:
time: 355 us; the launch traced here: 354 us
  waiting for transfers between devices  185 us (52%)
  local copies, waits for them, and re-layouts  55.2 us (16%)
  other arithmetic  50.8 us (14%)
  starting transfers between devices  31.6 us (9%)
  matrix products  16.1 us (5%)
  between operations  14.6 us (4%)
    psum x1, waiting for transfers between devices, per_device(): grad_wtemp = lax.psum(share, 'dom').astype(jnp.float32)  147 us
    unnamed x5, other arithmetic  18.8 us
    all_to_all x1, waiting for transfers between devices, per_device(): lax.all_to_all(tiles, 'dom', split_axis=0, concat_axis=0, tiled=True)  16.1 us
    all_to_all x1, starting transfers between devices, per_device(): lax.all_to_all(tiles, 'dom', split_axis=0, concat_axis=0, tiled=True)  13.3 us
    all_to_all x1, waiting for transfers between devices, per_device(): lax.all_to_all(halo_back.astype(jnp.bfloat16), 'dom', split_axis=0, conca...  11.1 us
    reshape x2, local copies, waits for them, and re-layouts, struct_core(): vals_g = val_tab[links].reshape(row_count, slots, HEADS, head_dim)  8.76 us
    reshape x2, local copies, waits for them, and re-layouts, struct_core(): keys_g = key_tab[links].reshape(row_count, slots, HEADS, head_dim)  8.71 us
    unnamed x51, local copies, waits for them, and re-layouts  7.9 us
  transfers between devices with their start and end apart: 6, of which 5 were waited for; matrix products, arithmetic and copies ran while one was open for 16% of the time, Pallas kernels for 0%

commit v1 on v0

v1 whole, which is shorter than its diff:
```python
import functools

import jax
import jax.numpy as jnp
from jax import lax
from jax.experimental import pallas as pl
from jax.experimental.pallas import tpu as pltpu
from jax.sharding import PartitionSpec as P

HEADS = 8
MESH = pl.DeviceIdType.MESH
BF = jnp.bfloat16
F32 = jnp.float32
GRID = {32: (8, 4), 4: (2, 2)}


def mm(a, b):
    return jnp.dot(a, b, preferred_element_type=F32)


def mm_nt(a, b):
    return lax.dot_general(a, b, (((1,), (1,)), ((), ())), preferred_element_type=F32)


def mm_tn(a, b):
    return lax.dot_general(a, b, (((0,), (0,)), ((), ())), preferred_element_type=F32)


def iota(shape, axis):
    return lax.broadcasted_iota(jnp.int32, shape, axis)


def where_bf(mask, value):
    return jnp.where(mask, value, jnp.zeros_like(value))


def copy_to(src, dst, send_sem, recv_sem, device):
    return pltpu.make_async_remote_copy(
        src_ref=src,
        dst_ref=dst,
        send_sem=send_sem,
        recv_sem=recv_sem,
        device_id=device,
        device_id_type=MESH,
    )


class Exchange:
    def __init__(self, count, me, device_of, src, dst, sems):
        self.count, self.me, self.device_of = count, me, device_of
        self.src, self.dst, self.send, self.recv = src, dst, sems.at[0], sems.at[1]

    def each(self, act):
        def body(step, carry):
            peer = lax.rem(self.me + step, self.count)
            act(peer)
            return carry

        lax.fori_loop(1, self.count, body, 0)

    def start(self):
        self.each(
            lambda peer: copy_to(
                self.src(peer),
                self.dst.at[self.me],
                self.send.at[peer],
                self.recv.at[self.me],
                self.device_of(peer),
            ).start()
        )

    def wait_recv(self):
        self.each(
            lambda peer: copy_to(
                self.src(peer),
                self.dst.at[peer],
                self.send.at[peer],
                self.recv.at[peer],
                self.device_of(peer),
            ).wait_recv()
        )

    def wait_send(self):
        self.each(
            lambda peer: copy_to(
                self.src(peer),
                self.dst.at[peer],
                self.send.at[peer],
                self.recv.at[peer],
                self.device_of(peer),
            ).wait_send()
        )


def kernel(
    sizes,
    x_ref,
    ws_ref,
    wt_ref,
    pos_ref,
    rb_ref,
    nbr_ref,
    rel_ref,
    send_ref,
    act_ref,
    ct_ref,
    out_ref,
    gw_ref,
    halo_s,
    halo_r,
    hid_s,
    hid_r,
    dh_s,
    dh_r,
    back_s,
    back_r,
    zt,
    zt_p,
    dt,
    dt_p,
    gx_s,
    gx_r,
    gy_s,
    gy_r,
    gz_s,
    gz_r,
    ga_r,
    q_ref,
    ktab,
    vtab,
    cmat,
    attn,
    agg_ref,
    dq_ref,
    dkv,
    tp,
    halo_sem,
    hid_sem,
    dh_sem,
    back_sem,
    pair_sem,
    gx_sem,
    gy_sem,
    gz_sem,
    ga_sem,
):
    nz, nx, ny = sizes
    n_dom, n_snap = nz * nx, 2 * ny
    rows, width = x_ref.shape
    halo = n_dom * 8
    table = rows + halo
    block = rows // n_snap
    cols = 3 * width // nx
    scale = (width // HEADS) ** -0.5

    me_d = lax.axis_index("dom")
    me_s = lax.axis_index("snap")
    me_z, me_x = me_d // nx, lax.rem(me_d, nx)
    me_y, me_c = me_s // 2, lax.rem(me_s, 2)
    partner = {"snap": me_s + 1 - 2 * me_c}

    barrier = pltpu.get_barrier_semaphore()

    def greet_dom(step, carry):
        pl.semaphore_signal(
            barrier, inc=1, device_id={"dom": lax.rem(me_d + step, n_dom)}, device_id_type=MESH
        )
        return carry

    def greet_snap(step, carry):
        pl.semaphore_signal(
            barrier, inc=1, device_id={"snap": lax.rem(me_s + step, n_snap)}, device_id_type=MESH
        )
        return carry

    lax.fori_loop(1, n_dom, greet_dom, 0)
    lax.fori_loop(1, n_snap, greet_snap, 0)

    halo_x = Exchange(
        n_dom, me_d, lambda p: {"dom": p}, lambda p: halo_s.at[p], halo_r, halo_sem
    )
    hid_x = Exchange(n_snap, me_s, lambda p: {"snap": p}, lambda p: hid_s.at[p], hid_r, hid_sem)
    dh_x = Exchange(n_snap, me_s, lambda p: {"snap": p}, lambda p: dh_s.at[p], dh_r, dh_sem)
    back_x = Exchange(
        n_dom, me_d, lambda p: {"dom": p}, lambda p: back_s.at[p], back_r, back_sem
    )
    gx_x = Exchange(
        nx, me_x, lambda p: {"dom": me_z * nx + p}, lambda p: gx_s.at[p], gx_r, gx_sem
    )
    gy_x = Exchange(
        ny, me_y, lambda p: {"snap": p * 2 + me_c}, lambda p: gy_s.at[p], gy_r, gy_sem
    )
    gz_x = Exchange(nz, me_z, lambda p: {"dom": p * nx + me_x}, lambda p: gz_s, gz_r, gz_sem)
    ga_x = Exchange(
        nx, me_x, lambda p: {"dom": me_z * nx + p}, lambda p: ga_r.at[me_x], ga_r, ga_sem
    )

    send_f = send_ref[...].astype(F32).astype(BF)
    spread = (lax.rem(iota((8, halo), 1), 8) == iota((8, halo), 0)).astype(F32).astype(BF)
    wide = mm(send_f, spread)
    picked = jnp.where(iota((n_dom, halo), 1) // 8 == iota((n_dom, halo), 0), wide, 0.0)
    send_row = jnp.sum(picked, axis=0, keepdims=True)
    pick_t = (iota((rows, halo), 0).astype(F32) == send_row).astype(F32)
    x_val = x_ref[...]
    tiles = mm(pick_t.T.astype(BF), x_val)
    halo_s[...] = tiles.reshape(n_dom, 8, width).astype(BF)

    pl.semaphore_wait(barrier, n_dom + n_snap - 2)
    halo_x.start()
    halo_r[me_d] = halo_s[me_d]

    own = mm(x_val, ws_ref[...]).astype(BF)
    q_ref[...] = own[:, :width]
    ktab[0:rows, :] = own[:, width : 2 * width]
    vtab[0:rows, :] = own[:, 2 * width :]

    nbr = nbr_ref[...]
    place = 1 << (4 * rel_ref[...])
    lane_t = iota((rows, table), 1)
    packed = jnp.zeros((rows, table), jnp.int32)
    for k in range(nbr.shape[1]):
        packed += jnp.where(lane_t == nbr[:, k : k + 1], place[:, k : k + 1], 0)
    counts = [((packed >> (4 * r)) & 15).astype(F32) for r in range(4)]
    eb = jnp.exp(rb_ref[...])
    for h in range(HEADS):
        total = counts[0] * eb[0:1, h : h + 1]
        for r in range(1, 4):
            total += counts[r] * eb[r : r + 1, h : h + 1]
        cmat[h] = total

    row_i = iota((rows, rows), 0)
    col_i = iota((rows, rows), 1)
    act_f = act_ref[...].astype(F32).astype(BF)
    over = (lax.rem(iota((block, rows), 1), block) == iota((block, rows), 0)).astype(F32)
    act_w = mm(act_f, over.astype(BF))
    act_row = jnp.sum(
        jnp.where(iota((n_snap, rows), 1) // block == iota((n_snap, rows), 0), act_w, 0.0),
        axis=0,
        keepdims=True,
    )
    same = lax.rem(row_i, block) == lax.rem(col_i, block)
    earlier = jnp.where(col_i // block <= row_i // block, act_row, 0.0)
    allowed = jnp.where(row_i == col_i, 1.0, jnp.where(same, earlier, 0.0))
    step_1h = (iota((rows, n_snap), 0) // block == iota((rows, n_snap), 1)).astype(F32)
    pos_rows = mm(step_1h.astype(BF), pos_ref[...])

    halo_x.wait_recv()
    halo_rows = halo_r[...].astype(F32).reshape(halo, width).astype(BF)
    ktab[rows:, :] = mm(halo_rows, ws_ref[:, width : 2 * width]).astype(BF)
    vtab[rows:, :] = mm(halo_rows, ws_ref[:, 2 * width :]).astype(BF)

    half = iota((rows, 128), 1) < 64
    halves = (half, jnp.logical_not(half))
    pairs = HEADS // 2

    for p in range(pairs):
        at = slice(128 * p, 128 * p + 128)
        q_p, k_p, v_p = q_ref[:, at], ktab[:, at], vtab[:, at]
        outs = []
        for s in range(2):
            score = mm_nt(where_bf(halves[s], q_p), k_p) * scale
            c = cmat[2 * p + s]
            score = jnp.where(c > 0, score, -1e30)
            e = jnp.exp(score - jnp.max(score, axis=1, keepdims=True)) * c
            w = e / jnp.sum(e, axis=1, keepdims=True)
            attn[2 * p + s] = w
            outs.append(mm(w.astype(BF), v_p))
        agg_ref[:, at] = jnp.where(half, outs[0], outs[1])
    agg = agg_ref[...]
    hidden = x_val.astype(F32) + jnp.where(agg > 0, agg, jnp.exp(jnp.minimum(agg, 0.0)) - 1.0)
    hid_s[...] = hidden.reshape(n_snap, block, width).astype(BF)
    hid_x.start()
    hid_r[me_s] = hid_s[me_s]

    ct_f = ct_ref[...].astype(F32).reshape(rows, width)
    ct = ct_f.astype(BF)
    hid_x.wait_recv()
    z_f = hid_r[...].astype(F32).reshape(rows, width).astype(F32) + pos_rows
    z = z_f.astype(BF)
    tp[...] = mm(z, wt_ref[...]).astype(BF)
    zt[...] = z_f.T.astype(BF).reshape(ny, 2, width // n_snap, rows)
    for p in range(pairs):
        at = slice(128 * p, 128 * p + 128)
        q_p = tp[:, 128 * p : 128 * p + 128]
        k_p = tp[:, width + 128 * p : width + 128 * p + 128]
        v_p = tp[:, 2 * width + 128 * p : 2 * width + 128 * p + 128]
        ct_p = ct[:, at]
        parts = []
        for s in range(2):
            score = mm_nt(where_bf(halves[s], q_p), k_p) * scale
            score = jnp.where(allowed > 0, score, -1e30)
            e = jnp.exp(score - jnp.max(score, axis=1, keepdims=True))
            w = e / jnp.sum(e, axis=1, keepdims=True)
            d_w = mm_nt(where_bf(halves[s], ct_p), v_p)
            t = w * d_w
            d_s = (t - w * jnp.sum(t, axis=1, keepdims=True)) * scale
            parts.append(
                (mm(d_s.astype(BF), k_p), mm(d_s.T.astype(BF), q_p), mm(w.T.astype(BF), ct_p))
            )
        for i in range(3):
            dt[:, width * i + 128 * p : width * i + 128 * p + 128] = jnp.where(
                half, parts[0][i], parts[1][i]
            ).astype(BF)

    pair_z = copy_to(
        zt.at[:, 1 - me_c], zt_p, pair_sem.at[0, 0], pair_sem.at[1, 0], partner
    )
    pair_d = copy_to(dt, dt_p, pair_sem.at[0, 1], pair_sem.at[1, 1], partner)
    pair_z.start()
    pair_d.start()

    d_z = ct_f + mm_nt(dt[...], wt_ref[...])
    dh_s[...] = d_z.reshape(n_snap, block, width).astype(BF)
    dh_x.start()
    dh_r[me_s] = dh_s[me_s]

    pair_z.wait_recv()
    pair_d.wait_recv()
    z_both = jnp.concatenate(
        [zt[:, me_c].reshape(width // 2, rows), zt_p[...].reshape(width // 2, rows)], axis=1
    )
    for i in range(nx):
        cut = slice(cols * i, cols * i + cols)
        d_both = jnp.concatenate([dt[:, cut], dt_p[:, cut]], axis=0)
        gx_s[i] = mm(z_both, d_both).astype(BF)
    gx_x.start()

    dh_x.wait_recv()
    dh_f = dh_r[...].astype(F32).reshape(rows, width)
    agg = agg_ref[...]
    d_agg = dh_f * jnp.where(agg > 0, 1.0, jnp.exp(jnp.minimum(agg, 0.0)))
    d_agg = d_agg.astype(BF)
    half_t = iota((table, 128), 1) < 64
    for p in range(pairs):
        at = slice(128 * p, 128 * p + 128)
        q_p, k_p, v_p = q_ref[:, at], ktab[:, at], vtab[:, at]
        da_p = d_agg[:, at]
        parts = []
        for s in range(2):
            w = attn[2 * p + s]
            d_w = mm_nt(where_bf(halves[s], da_p), v_p)
            t = w * d_w
            d_s = (t - w * jnp.sum(t, axis=1, keepdims=True)) * scale
            parts.append(
                (mm(d_s.astype(BF), k_p), mm(d_s.T.astype(BF), q_p), mm(w.T.astype(BF), da_p))
            )
        dq_ref[:, at] = jnp.where(half, parts[0][0], parts[1][0]).astype(BF)
        dkv[:, at] = jnp.where(half_t, parts[0][1], parts[1][1]).astype(BF)
        dkv[:, width + 128 * p : width + 128 * p + 128] = jnp.where(
            half_t, parts[0][2], parts[1][2]
        ).astype(BF)

    d_halo = mm_nt(dkv[rows:, :], ws_ref[:, width:])
    back_s[...] = d_halo.reshape(n_dom, 8, width).astype(BF)
    back_x.start()
    back_r[me_d] = back_s[me_d]

    gx_x.wait_recv()
    gx_r[me_x] = gx_s[me_x]
    total = gx_r[0].astype(F32)
    for i in range(1, nx):
        total += gx_r[i].astype(F32)
    gy_s[...] = total.astype(BF).reshape(ny, width // n_snap, cols)
    gy_x.start()

    d_own = dh_f + mm_nt(dq_ref[...], ws_ref[:, :width]) + mm_nt(dkv[0:rows, :], ws_ref[:, width:])

    gy_x.wait_recv()
    gy_r[me_y] = gy_s[me_y]
    total = gy_r[0].astype(F32)
    for i in range(1, ny):
        total += gy_r[i].astype(F32)
    gz_s[...] = total.astype(BF)
    gz_x.start()
    gz_r[me_z] = gz_s[...]

    back_x.wait_recv()
    came = back_r[...].astype(F32).reshape(halo, width).astype(BF)
    out_ref[...] = (d_own + mm(pick_t.astype(BF), came)).astype(BF)

    gz_x.wait_recv()
    total = gz_r[0].astype(F32)
    for i in range(1, nz):
        total += gz_r[i].astype(F32)
    ga_r[me_x] = total.astype(BF)
    ga_x.start()
    ga_x.wait_recv()
    for i in range(nx):
        gw_ref[:, cols * i : cols * i + cols] = ga_r[i].astype(F32)

    for exchange in (halo_x, hid_x, dh_x, back_x, gx_x, gy_x, gz_x, ga_x):
        exchange.wait_send()
    pair_z.wait_send()
    pair_d.wait_send()


def per_device(
    feat, w_struct, w_temp, pos_embed, rel_bias, nbr, rel_type, send_idx, active, cotangent
):
    x = feat[0]
    rows, width = x.shape
    n_dom, n_snap = lax.axis_size("dom"), lax.axis_size("snap")
    nz, nx = GRID[n_dom]
    ny = n_snap // 2
    halo = n_dom * 8
    table = rows + halo
    block = rows // n_snap
    cols = 3 * width // nx
    wrows = width // n_snap
    vm = pltpu.VMEM
    dma = pltpu.SemaphoreType.DMA
    scratch = [
        vm((n_dom, 8, width), BF),
        vm((n_dom, 8, width), BF),
        vm((n_snap, block, width), BF),
        vm((n_snap, block, width), BF),
        vm((n_snap, block, width), BF),
        vm((n_snap, block, width), BF),
        vm((n_dom, 8, width), BF),
        vm((n_dom, 8, width), BF),
        vm((ny, 2, wrows, rows), BF),
        vm((ny, wrows, rows), BF),
        vm((rows, 3 * width), BF),
        vm((rows, 3 * width), BF),
        vm((nx, width // 2, cols), BF),
        vm((nx, width // 2, cols), BF),
        vm((ny, wrows, cols), BF),
        vm((ny, wrows, cols), BF),
        vm((wrows, cols), BF),
        vm((nz, wrows, cols), BF),
        vm((nx, wrows, cols), BF),
        vm((rows, width), BF),
        vm((table, width), BF),
        vm((table, width), BF),
        vm((HEADS, rows, table), F32),
        vm((HEADS, rows, table), F32),
        vm((rows, width), F32),
        vm((rows, width), BF),
        vm((table, 2 * width), BF),
        vm((rows, 3 * width), BF),
        dma((2, n_dom)),
        dma((2, n_snap)),
        dma((2, n_snap)),
        dma((2, n_dom)),
        dma((2, 2)),
        dma((2, nx)),
        dma((2, ny)),
        dma((2, nz)),
        dma((2, nx)),
    ]
    grad, gw = pl.pallas_call(
        functools.partial(kernel, (nz, nx, ny)),
        out_shape=(
            jax.ShapeDtypeStruct((rows, width), BF),
            jax.ShapeDtypeStruct((wrows, 3 * width), F32),
        ),
        in_specs=[pl.BlockSpec(memory_space=pltpu.VMEM)] * 10,
        out_specs=(pl.BlockSpec(memory_space=pltpu.VMEM),) * 2,
        scratch_shapes=scratch,
        compiler_params=pltpu.CompilerParams(collective_id=0, has_side_effects=True),
        name="step",
    )(
        x,
        w_struct,
        w_temp,
        pos_embed,
        rel_bias,
        nbr[0],
        rel_type[0],
        send_idx[0, 0],
        active,
        cotangent,
    )
    return (grad[None], gw)


def solution(mesh):
    return jax.shard_map(
        per_device,
        mesh=mesh,
        in_specs=(
            P("snap", "dom", None),
            P(),
            P(),
            P(),
            P(),
            P("snap", "dom", None),
            P("snap", "dom", None),
            P("snap", "dom", None, None),
            P(None, ("dom", "snap")),
            P(None, ("dom", "snap"), None),
        ),
        out_specs=(P("snap", "dom", None), P("snap", None)),
        check_vma=False,
    )
```

time: 355 us -> 83.6 us (0.24)
  the two profiles are of different devices: /device:TPU:24 before, /device:TPU:32 now
where the time goes in v1:
time: 83.6 us; the launch traced here: 83.3 us
  Pallas kernels  74 us (89%)
  local copies, waits for them, and re-layouts  8.72 us (10%)
    pallas_call x1, Pallas kernels, per_device(): pl.pallas_call(functools.partial(kernel, (nz, nx, ny)), out_shape=(jax.Sh...  74 us
    unnamed x6, local copies, waits for them, and re-layouts  8.72 us

profile of v1, /device:TPU:32, one launch (start us, length us, event | category | flops | bytes accessed | tf_op | source)
XLA Modules:
  0.0 83.3 jit_solution(7810538539399901518)
XLA Ops:
  0.6 1.3 %copy.15.act_ref = s32[16,8]{1,0:T(8,128)} copy(s32[16,8]{0,1:T(8,128)} %param.18) | data formatting | bytes 1024 | tf_op args[8]
  2.0 1.4 %copy.14 = s32[1,1,32,8]{3,2,1,0:T(8,128)} copy(s32[1,1,32,8]{2,3,1,0:T(8,128)} %param.17) | data formatting | bytes 2048 | tf_op args[7]
  3.3 1.4 %copy.12 = s32[1,128,8]{2,1,0:T(8,128)} copy(s32[1,128,8]{1,2,0:T(8,128)} %param.15) | data formatting | bytes 8192 | tf_op args[5]
  4.8 1.4 %copy.13 = s32[1,128,8]{2,1,0:T(8,128)} copy(s32[1,128,8]{1,2,0:T(8,128)} %param.16) | data formatting | bytes 8192 | tf_op args[6]
  6.2 74.0 %step.1 = (bf16[128,512]{1,0:T(8,128)(2,1)}, f32[32,1536]{1,0:T(8,128)}) custom-call(bf16[128,512]{1,0:T(8,128)(2,1)} %bitcast.7, bf16[512,1536]{1,0:T(8,128)(2,1)} %ws_ref.1, bf16[512,1536]{1,0:T(8,128)(2,1)} %wt_ref.1, bf16[16,512]{1,0:T(8,128)(2,1)} %pos_ref.1, f32[4,8]{1,0:T(4,128)} %rb_ref.1, s32[128,8]{1,0:T(8,128)} %bitcast.5, s32[128,8]{1,0:T(8,128)} %bitcast.6, ...), custom_call_target="tpu_custom_call" | custom-call | tf_op jit(solution)/shard_map/step/pallas_call | solution.py:451
  80.2 1.6 %copy.18 = bf16[1,128,512]{2,1,0:T(8,128)(2,1)} copy(bf16[1,128,512]{2,1,0:T(8,128)(2,1)} %bitcast.8) | data formatting | bytes 262144
  81.7 1.6 %copy.19 = f32[32,1536]{1,0:T(8,128)} copy(f32[32,1536]{1,0:T(8,128)} %get-tuple-element.9) | data formatting | bytes 393216

commit v2 on v1

v2 whole, which is shorter than its diff:
```python
import functools

import jax
import jax.numpy as jnp
from jax import lax
from jax.experimental import pallas as pl
from jax.experimental.pallas import tpu as pltpu
from jax.sharding import PartitionSpec as P

HEADS = 8
MESH = pl.DeviceIdType.MESH
BF = jnp.bfloat16
F32 = jnp.float32
GRID = {32: (8, 4), 4: (2, 2), 8: (2, 4)}


def mm(a, b):
    return jnp.dot(a, b, preferred_element_type=F32)


def mm_nt(a, b):
    return lax.dot_general(a, b, (((1,), (1,)), ((), ())), preferred_element_type=F32)


def mm_tn(a, b):
    return lax.dot_general(a, b, (((0,), (0,)), ((), ())), preferred_element_type=F32)


def iota(shape, axis):
    return lax.broadcasted_iota(jnp.int32, shape, axis)


def where_bf(mask, value):
    return jnp.where(mask, value, jnp.zeros_like(value))


def copy_to(src, dst, send_sem, recv_sem, device):
    return pltpu.make_async_remote_copy(
        src_ref=src,
        dst_ref=dst,
        send_sem=send_sem,
        recv_sem=recv_sem,
        device_id=device,
        device_id_type=MESH,
    )


class Exchange:
    def __init__(self, count, me, device_of, src, dst, sems):
        self.count, self.me, self.device_of = count, me, device_of
        self.src, self.dst, self.send, self.recv = src, dst, sems.at[0], sems.at[1]

    def each(self, act):
        def body(step, carry):
            near = (step + 1) // 2
            shift = near + (step + 1) % 2 * (self.count - 2 * near)
            act(lax.rem(self.me + shift, self.count))
            return carry

        lax.fori_loop(1, self.count, body, 0)

    def start(self):
        self.each(
            lambda peer: copy_to(
                self.src(peer),
                self.dst.at[self.me],
                self.send.at[peer],
                self.recv.at[self.me],
                self.device_of(peer),
            ).start()
        )

    def wait_recv(self):
        self.each(
            lambda peer: copy_to(
                self.src(peer),
                self.dst.at[peer],
                self.send.at[peer],
                self.recv.at[peer],
                self.device_of(peer),
            ).wait_recv()
        )

    def wait_send(self):
        self.each(
            lambda peer: copy_to(
                self.src(peer),
                self.dst.at[peer],
                self.send.at[peer],
                self.recv.at[peer],
                self.device_of(peer),
            ).wait_send()
        )


def kernel(
    sizes,
    x_hbm,
    ws_hbm,
    wt_hbm,
    pos_hbm,
    rb_hbm,
    nbr_hbm,
    rel_hbm,
    send_hbm,
    act_hbm,
    ct_hbm,
    out_hbm,
    gw_hbm,
    x_ref,
    ws_ref,
    wt_ref,
    pos_ref,
    rb_ref,
    nbr_ref,
    rel_ref,
    send_ref,
    act_ref,
    ct_ref,
    in_sem,
    out_ref,
    gw_ref,
    out_sem,
    halo_s,
    halo_r,
    hid_s,
    hid_r,
    dh_s,
    dh_r,
    back_s,
    back_r,
    zt,
    zt_p,
    dt,
    dt_p,
    gx_s,
    gx_r,
    gx_v,
    xy_s,
    xy_r,
    xz_s,
    xz_r,
    xa_r,
    zz_s,
    zz_r,
    zy_s,
    zy_r,
    zx_r,
    za_r,
    qst,
    ktab,
    vtab,
    wvt,
    vt,
    ktt,
    cmat,
    attn,
    attn_b,
    d_att,
    d_sc,
    das,
    agg_t,
    slope,
    dkv,
    allow,
    pos_rows,
    cts,
    tp,
    tqs,
    t_s,
    t_d,
    t_w,
    t_b,
    halo_sem,
    hid_sem,
    dh_sem,
    back_sem,
    pair_sem,
    gx_sem,
    xy_sem,
    xz_sem,
    xa_sem,
    zz_sem,
    zy_sem,
    zx_sem,
    za_sem,
):
    nz, nx, ny = sizes
    n_dom, n_snap = nz * nx, 2 * ny
    rows, width = x_ref.shape
    halo = n_dom * 8
    table = rows + halo
    block = rows // n_snap
    cols = 2 * width // nx
    wrows = width // n_snap
    xrows, zc = wrows // (nz // 2), min(4, nz)
    zrows, zcols = wrows // (nz // zc), width // zc
    scale = (width // HEADS) ** -0.5
    scale_bf = jnp.asarray(scale, BF)
    pairs = HEADS // 2

    loads = {
        "send": (send_hbm, send_ref),
        "x": (x_hbm, x_ref),
        "ws": (ws_hbm, ws_ref),
        "nbr": (nbr_hbm, nbr_ref),
        "rel": (rel_hbm, rel_ref),
        "rb": (rb_hbm, rb_ref),
        "act": (act_hbm, act_ref),
        "pos": (pos_hbm, pos_ref),
        "ct": (ct_hbm, ct_ref),
        "wt": (wt_hbm, wt_ref),
    }
    order = list(loads)

    def input_copy(name):
        return pltpu.make_async_copy(*loads[name], in_sem.at[order.index(name)])

    def arrive(name, load=True):
        input_copy(name).wait()
        return loads[name][1][...] if load else None

    for name in order:
        input_copy(name).start()

    me_d = lax.axis_index("dom")
    me_s = lax.axis_index("snap")
    me_z, me_x = me_d // nx, lax.rem(me_d, nx)
    me_y, me_c = me_s // 2, lax.rem(me_s, 2)
    partner = {"snap": me_s + 1 - 2 * me_c}

    barrier = pltpu.get_barrier_semaphore()

    def greet_dom(step, carry):
        pl.semaphore_signal(
            barrier, inc=1, device_id={"dom": lax.rem(me_d + step, n_dom)}, device_id_type=MESH
        )
        return carry

    def greet_snap(step, carry):
        pl.semaphore_signal(
            barrier, inc=1, device_id={"snap": lax.rem(me_s + step, n_snap)}, device_id_type=MESH
        )
        return carry

    lax.fori_loop(1, n_dom, greet_dom, 0)
    lax.fori_loop(1, n_snap, greet_snap, 0)

    halo_x = Exchange(
        n_dom, me_d, lambda p: {"dom": p}, lambda p: halo_s.at[p], halo_r, halo_sem
    )
    hid_x = Exchange(n_snap, me_s, lambda p: {"snap": p}, lambda p: hid_s.at[p], hid_r, hid_sem)
    dh_x = Exchange(n_snap, me_s, lambda p: {"snap": p}, lambda p: dh_s.at[p], dh_r, dh_sem)
    back_x = Exchange(
        n_dom, me_d, lambda p: {"dom": p}, lambda p: back_s.at[p], back_r, back_sem
    )
    py_x = Exchange(
        ny, me_y, lambda p: {"snap": p * 2 + me_c}, lambda p: xy_s.at[p], xy_r, xy_sem
    )
    pz_x = Exchange(nz, me_z, lambda p: {"dom": p * nx + me_x}, lambda p: xz_s.at[p], xz_r, xz_sem)
    pa_x = Exchange(n_dom, me_d, lambda p: {"dom": p}, lambda p: xa_r.at[me_d], xa_r, xa_sem)
    qz_x = Exchange(nz, me_z, lambda p: {"dom": p * nx + me_x}, lambda p: zz_s.at[p], zz_r, zz_sem)
    qy_x = Exchange(
        ny, me_y, lambda p: {"snap": p * 2 + me_c}, lambda p: zy_s.at[p], zy_r, zy_sem
    )
    qx_x = Exchange(
        nx, me_x, lambda p: {"dom": me_z * nx + p}, lambda p: zx_r.at[me_x], zx_r, zx_sem
    )
    qa_x = Exchange(
        nz, me_z, lambda p: {"dom": p * nx + me_x}, lambda p: za_r.at[me_z], za_r, za_sem
    )
    right, left = lax.rem(me_x + 1, nx), lax.rem(me_x + nx - 1, nx)
    to_right, to_left = {"dom": me_z * nx + right}, {"dom": me_z * nx + left}
    mid = width // 4
    top, low = pl.ds(0, mid), pl.ds(mid, mid)

    def neighbour(src, dst, slot, device):
        return copy_to(src, dst, gx_sem.at[0, slot], gx_sem.at[1, slot], device)

    if nx == 4:
        across = lax.rem(me_x + 2, nx)
        hops = [
            neighbour(gx_s.at[across, top], gx_v.at[0], 0, to_right),
            neighbour(gx_s.at[across, low], gx_v.at[1], 1, to_left),
            neighbour(gx_s.at[right, low], gx_r.at[0, low], 2, to_right),
            neighbour(gx_s.at[left, top], gx_r.at[1, top], 3, to_left),
            neighbour(gx_v.at[2], gx_r.at[0, top], 4, to_right),
            neighbour(gx_v.at[3], gx_r.at[1, low], 5, to_left),
        ]
    else:
        hops = [neighbour(gx_s.at[right], gx_r.at[0], 0, to_right)]

    send_f = arrive("send").astype(F32).astype(BF)
    spread = (iota((n_dom, halo), 1) // 8 == iota((n_dom, halo), 0)).astype(F32).astype(BF)
    wide = mm(send_f, spread)
    picked = jnp.where(lax.rem(iota((8, halo), 1), 8) == iota((8, halo), 0), wide, 0.0)
    send_row = jnp.sum(picked, axis=0, keepdims=True)
    pick_t = (iota((rows, halo), 0).astype(F32) == send_row).astype(F32)
    pick = pick_t.T.astype(BF)
    x_val = arrive("x")
    tiles = mm(pick, x_val)
    halo_s[...] = tiles.reshape(n_dom, 8, width).astype(BF)

    pl.semaphore_wait(barrier, n_dom + n_snap - 2)
    halo_x.start()
    halo_r[me_d] = halo_s[me_d]

    half = iota((rows, 128), 1) < 64

    def stack(value):
        zero = jnp.zeros_like(value)
        return jnp.concatenate(
            [jnp.where(half, value, zero), jnp.where(half, zero, value)], axis=0
        )

    w_v = pl.ds(2 * width, width)
    arrive("ws", load=False)
    own = mm(x_val, ws_ref[...]).astype(BF)
    ktab[0:rows, :] = own[:, width : 2 * width]
    vtab[0:rows, :] = own[:, 2 * width :]
    for p in range(pairs):
        qst[p] = stack(own[:, 128 * p : 128 * p + 128] * scale_bf)
    wvt[...] = ws_ref[:, w_v].T
    vt[:, 0:rows] = mm_nt(wvt[...], x_val).astype(BF)

    nbr = arrive("nbr").astype(F32)
    slots = nbr.shape[0]
    place = (1 << (4 * arrive("rel"))).astype(F32)
    row_t = iota((table, rows), 0).astype(F32)
    packed = jnp.zeros((table, rows), F32)
    for k in range(slots):
        packed += jnp.where(row_t == nbr[k : k + 1, :], place[k : k + 1, :], 0.0)
    packed = packed.astype(jnp.int32)
    counts = [((packed >> (4 * r)) & 15).astype(F32) for r in range(4)]
    eb = jnp.exp(arrive("rb"))
    for h in range(HEADS):
        total = counts[0] * eb[0:1, h : h + 1]
        for r in range(1, 4):
            total += counts[r] * eb[r : r + 1, h : h + 1]
        cmat[h // 2, :, (h % 2) * rows : (h % 2) * rows + rows] = total

    row_i = iota((rows, rows), 0)
    col_i = iota((rows, rows), 1)
    act_f = arrive("act").astype(F32).astype(BF)
    over = (iota((n_snap, rows), 1) // block == iota((n_snap, rows), 0)).astype(F32)
    act_w = mm(act_f, over.astype(BF))
    act_own = lax.rem(iota((block, rows), 1), block) == iota((block, rows), 0)
    act_row = jnp.sum(jnp.where(act_own, act_w, 0.0), axis=0, keepdims=True)
    same = lax.rem(row_i, block) == lax.rem(col_i, block)
    earlier = jnp.where(col_i // block <= row_i // block, act_row, 0.0)
    allowed = jnp.where(row_i == col_i, 1.0, jnp.where(same, earlier, 0.0)).T
    allow[:, 0:rows] = allowed
    allow[:, rows:] = allowed
    step_1h = (iota((rows, n_snap), 0) // block == iota((rows, n_snap), 1)).astype(F32)
    pos_rows[...] = mm(step_1h.astype(BF), arrive("pos"))
    ct_f = arrive("ct").astype(F32).reshape(rows, width)
    ct = ct_f.astype(BF)
    for p in range(pairs):
        cts[p] = stack(ct[:, 128 * p : 128 * p + 128])

    halo_x.wait_recv()
    halo_rows = halo_r[...].astype(F32).reshape(halo, width).astype(BF)
    ktab[rows:, :] = mm(halo_rows, ws_ref[:, width : 2 * width]).astype(BF)
    vt[:, rows:] = mm_nt(wvt[...], halo_rows).astype(BF)

    for p in range(pairs):
        attn[p] = mm_nt(ktab[:, 128 * p : 128 * p + 128], qst[p])
    for p in range(pairs):
        c = cmat[p]
        score = jnp.where(c > 0, attn[p], -1e30)
        e = jnp.exp(score - jnp.max(score, axis=0, keepdims=True)) * c
        w = e * (1.0 / jnp.sum(e, axis=0, keepdims=True))
        attn[p] = w
        attn_b[p] = w.astype(BF)
    for p in range(pairs):
        o = mm(vt[128 * p : 128 * p + 128, :], attn_b[p])
        agg_t[128 * p : 128 * p + 64, :] = o[0:64, 0:rows]
        agg_t[128 * p + 64 : 128 * p + 128, :] = o[64:128, rows:]
    agg = agg_t[...].T
    hidden = x_val.astype(F32) + jnp.where(agg > 0, agg, jnp.exp(jnp.minimum(agg, 0.0)) - 1.0)
    hid_s[...] = hidden.reshape(n_snap, block, width).astype(BF)
    hid_x.start()
    hid_r[me_s] = hid_s[me_s]
    slope[...] = jnp.where(agg > 0, 1.0, jnp.exp(jnp.minimum(agg, 0.0)))
    vtab[rows:, :] = mm(halo_rows, ws_ref[:, w_v]).astype(BF)
    ktt[...] = ktab[...].T
    arrive("wt", load=False)
    halo_x.wait_send()

    hid_x.wait_recv()
    z_f = hid_r[...].astype(F32).reshape(rows, width) + pos_rows[...]
    z = z_f.astype(BF)
    tp[...] = mm(z, wt_ref[...]).astype(BF)
    zt[...] = z_f.T.astype(BF).reshape(ny, 2, width // n_snap, rows)
    for p in range(pairs):
        tqs[p] = stack(tp[:, 128 * p : 128 * p + 128] * scale_bf)
        t_s[p] = mm_nt(tp[:, width + 128 * p : width + 128 * p + 128], tqs[p])
        t_d[p] = mm_nt(tp[:, 2 * width + 128 * p : 2 * width + 128 * p + 128], cts[p])
    for p in range(pairs):
        score = jnp.where(allow[...] > 0, t_s[p], -1e30)
        e = jnp.exp(score - jnp.max(score, axis=0, keepdims=True))
        w = e * (1.0 / jnp.sum(e, axis=0, keepdims=True))
        t = w * t_d[p]
        t_w[p] = w.astype(BF)
        t_b[p] = (t - w * jnp.sum(t, axis=0, keepdims=True)).astype(BF)
    for p in range(pairs):
        at = 128 * p
        dq = mm_tn(t_b[p], tp[:, width + at : width + at + 128]) * scale
        dt[:, at : at + 128] = jnp.where(half, dq[0:rows], dq[rows:]).astype(BF)
        dt[:, width + at : width + at + 128] = mm(t_b[p], tqs[p]).astype(BF)
        dt[:, 2 * width + at : 2 * width + at + 128] = mm(t_w[p], cts[p]).astype(BF)

    pair_z = copy_to(
        zt.at[:, 1 - me_c], zt_p, pair_sem.at[0, 0], pair_sem.at[1, 0], partner
    )
    pair_d = copy_to(dt, dt_p, pair_sem.at[0, 1], pair_sem.at[1, 1], partner)
    pair_z.start()
    pair_d.start()

    d_z = ct_f + mm_nt(dt[...], wt_ref[...])
    dh_s[...] = d_z.reshape(n_snap, block, width).astype(BF)
    dh_x.start()
    dh_r[me_s] = dh_s[me_s]

    pair_z.wait_recv()
    pair_d.wait_recv()
    z_both = jnp.concatenate(
        [zt[:, me_c].reshape(width // 2, rows), zt_p[...].reshape(width // 2, rows)], axis=1
    )
    d_both = jnp.concatenate([dt[:, 0 : 2 * width], dt_p[:, 0 : 2 * width]], axis=0)
    for i in range(nx):
        gx_s[i] = mm(z_both, d_both[:, cols * i : cols * i + cols]).astype(BF)
    d_both = jnp.concatenate([dt[:, 2 * width :], dt_p[:, 2 * width :]], axis=0)
    product = mm(z_both, d_both).reshape(ny, wrows, width)
    for i in range(nz):
        r, c = i // zc * zrows, i % zc * zcols
        zz_s[i] = product[:, r : r + zrows, c : c + zcols].astype(BF)
    for hop in hops[0:4]:
        hop.start()
    qz_x.start()
    zz_r[me_z] = zz_s[me_z]
    if nx == 4:
        hops[0].wait_recv()
        hops[1].wait_recv()
        gx_v[2] = (gx_s[right, top].astype(F32) + gx_v[0].astype(F32)).astype(BF)
        gx_v[3] = (gx_s[left, low].astype(F32) + gx_v[1].astype(F32)).astype(BF)
        hops[4].start()
        hops[5].start()

    hid_x.wait_send()
    dh_x.wait_recv()
    dh_f = dh_r[...].astype(F32).reshape(rows, width)
    d_agg = (dh_f * slope[...]).astype(BF)
    for p in range(pairs):
        das[p] = stack(d_agg[:, 128 * p : 128 * p + 128])
        d_att[p] = mm_nt(vtab[:, 128 * p : 128 * p + 128], das[p])
    for p in range(pairs):
        w = attn[p]
        t = w * d_att[p]
        d_sc[p] = (t - w * jnp.sum(t, axis=0, keepdims=True)).astype(BF)
    for p in range(pairs):
        at = 128 * p
        dkv[rows:, at : at + 128] = mm(d_sc[p, rows:, :], qst[p]).astype(BF)
        dkv[rows:, width + at : width + at + 128] = mm(attn_b[p, rows:, :], das[p]).astype(BF)

    d_halo = mm_nt(dkv[rows:, :], ws_ref[:, width:])
    back_s[...] = d_halo.reshape(n_dom, 8, width).astype(BF)
    back_x.start()
    back_r[me_d] = back_s[me_d]

    for hop in hops[2:] if nx == 4 else hops:
        hop.wait_recv()
    total = gx_s[me_x].astype(F32) + gx_r[0].astype(F32)
    if nx == 4:
        total += gx_r[1].astype(F32)
    xy_s[...] = total.astype(BF).reshape(ny, wrows, cols)
    py_x.start()
    xy_r[me_y] = xy_s[me_y]

    for p in range(pairs):
        at = 128 * p
        dkv[0:rows, at : at + 128] = mm(d_sc[p, 0:rows, :], qst[p]).astype(BF)
        dkv[0:rows, width + at : width + at + 128] = mm(attn_b[p, 0:rows, :], das[p]).astype(BF)
        o = mm(ktt[at : at + 128, :], d_sc[p]) * scale
        agg_t[at : at + 64, :] = o[0:64, 0:rows]
        agg_t[at + 64 : at + 128, :] = o[64:128, rows:]
    dq = agg_t[...].T.astype(BF)
    d_own = dh_f + mm_nt(dq, ws_ref[:, :width]) + mm_nt(dkv[0:rows, :], ws_ref[:, width:])
    dh_x.wait_send()
    pair_z.wait_send()
    pair_d.wait_send()
    for hop in hops:
        hop.wait_send()

    def total_of(ref, count):
        total = ref[0].astype(F32)
        for i in range(1, count):
            total += ref[i].astype(F32)
        return total

    qz_x.wait_recv()
    zy_s[...] = total_of(zz_r, nz).astype(BF)
    qy_x.start()
    zy_r[me_y] = zy_s[me_y]

    py_x.wait_recv()
    total = total_of(xy_r, ny)
    for i in range(nz):
        r, c = i // 2 * xrows, i % 2 * 128
        xz_s[i] = total[r : r + xrows, c : c + 128].astype(BF)
    pz_x.start()
    xz_r[me_z] = xz_s[me_z]
    qz_x.wait_send()
    py_x.wait_send()

    qy_x.wait_recv()
    zx_r[me_x] = total_of(zy_r, ny).astype(BF)
    qx_x.start()
    qy_x.wait_send()

    back_x.wait_recv()
    came = back_r[...].astype(F32).reshape(halo, width).astype(BF)
    out_ref[...] = (d_own + mm(pick_t.astype(BF), came)).astype(BF)
    save_out = pltpu.make_async_copy(out_ref, out_hbm, out_sem.at[0])
    save_out.start()

    pz_x.wait_recv()
    xa_r[me_d] = total_of(xz_r, nz).astype(BF)
    pa_x.start()
    qx_x.wait_recv()
    za_r[me_z] = total_of(zx_r, nx).astype(BF)
    qa_x.start()
    back_x.wait_send()
    pz_x.wait_send()
    qx_x.wait_send()
    qa_x.wait_recv()
    for i in range(nz):
        r, c = i // zc * zrows, 2 * width + i % zc * zcols
        gw_ref[r : r + zrows, c : c + zcols] = za_r[i].astype(F32)
    pa_x.wait_recv()
    for i in range(n_dom):
        r, c = i // nx // 2 * xrows, i % nx * cols + i // nx % 2 * 128
        gw_ref[r : r + xrows, c : c + 128] = xa_r[i].astype(F32)
    save_gw = pltpu.make_async_copy(gw_ref, gw_hbm, out_sem.at[1])
    save_gw.start()
    pa_x.wait_send()
    qa_x.wait_send()
    save_out.wait()
    save_gw.wait()


def emit(grad_ref, gw_ref, grad_out, gw_out):
    grad_out[...] = grad_ref[...]
    gw_out[...] = gw_ref[...]


def per_device(
    feat, w_struct, w_temp, pos_embed, rel_bias, nbr, rel_type, send_idx, active, cotangent
):
    x = feat[0]
    rows, width = x.shape
    n_dom, n_snap = lax.axis_size("dom"), lax.axis_size("snap")
    nz, nx = GRID[n_dom]
    ny = n_snap // 2
    halo = n_dom * 8
    table = rows + halo
    block = rows // n_snap
    cols = 2 * width // nx
    wrows = width // n_snap
    xrows, zc = wrows // (nz // 2), min(4, nz)
    zrows, zcols = wrows // (nz // zc), width // zc
    vm = pltpu.VMEM
    dma = pltpu.SemaphoreType.DMA
    arrays = (
        x,
        w_struct,
        w_temp,
        pos_embed,
        rel_bias,
        nbr[0].T,
        rel_type[0].T,
        send_idx[0, 0].T,
        active.T,
        cotangent,
    )
    pairs = HEADS // 2
    scratch = [vm(a.shape, a.dtype) for a in arrays] + [
        dma((len(arrays),)),
        vm((rows, width), BF),
        vm((wrows, 3 * width), F32),
        dma((2,)),
        vm((n_dom, 8, width), BF),
        vm((n_dom, 8, width), BF),
        vm((n_snap, block, width), BF),
        vm((n_snap, block, width), BF),
        vm((n_snap, block, width), BF),
        vm((n_snap, block, width), BF),
        vm((n_dom, 8, width), BF),
        vm((n_dom, 8, width), BF),
        vm((ny, 2, wrows, rows), BF),
        vm((ny, wrows, rows), BF),
        vm((rows, 3 * width), BF),
        vm((rows, 3 * width), BF),
        vm((nx, width // 2, cols), BF),
        vm((2, width // 2, cols), BF),
        vm((4, width // 4, cols), BF),
        vm((ny, wrows, cols), BF),
        vm((ny, wrows, cols), BF),
        vm((nz, xrows, 128), BF),
        vm((nz, xrows, 128), BF),
        vm((n_dom, xrows, 128), BF),
        vm((nz, ny, zrows, zcols), BF),
        vm((nz, ny, zrows, zcols), BF),
        vm((ny, zrows, zcols), BF),
        vm((ny, zrows, zcols), BF),
        vm((nx, zrows, zcols), BF),
        vm((nz, zrows, zcols), BF),
        vm((pairs, 2 * rows, 128), BF),
        vm((table, width), BF),
        vm((table, width), BF),
        vm((width, width), BF),
        vm((width, table), BF),
        vm((width, table), BF),
        vm((pairs, table, 2 * rows), F32),
        vm((pairs, table, 2 * rows), F32),
        vm((pairs, table, 2 * rows), BF),
        vm((pairs, table, 2 * rows), F32),
        vm((pairs, table, 2 * rows), BF),
        vm((pairs, 2 * rows, 128), BF),
        vm((width, rows), F32),
        vm((rows, width), F32),
        vm((table, 2 * width), BF),
        vm((rows, 2 * rows), F32),
        vm((rows, width), F32),
        vm((pairs, 2 * rows, 128), BF),
        vm((rows, 3 * width), BF),
        vm((pairs, 2 * rows, 128), BF),
        vm((pairs, rows, 2 * rows), F32),
        vm((pairs, rows, 2 * rows), F32),
        vm((pairs, rows, 2 * rows), BF),
        vm((pairs, rows, 2 * rows), BF),
        dma((2, n_dom)),
        dma((2, n_snap)),
        dma((2, n_snap)),
        dma((2, n_dom)),
        dma((2, 2)),
        dma((2, 6)),
        dma((2, ny)),
        dma((2, nz)),
        dma((2, n_dom)),
        dma((2, nz)),
        dma((2, ny)),
        dma((2, nx)),
        dma((2, nz)),
    ]
    in_vmem = pl.BlockSpec(memory_space=pltpu.VMEM)
    in_any = pl.BlockSpec(memory_space=pl.ANY)
    grad, gw = pl.pallas_call(
        functools.partial(kernel, (nz, nx, ny)),
        out_shape=(
            jax.ShapeDtypeStruct((rows, width), BF),
            jax.ShapeDtypeStruct((wrows, 3 * width), F32),
        ),
        in_specs=[in_any] * len(arrays),
        out_specs=(in_any,) * 2,
        scratch_shapes=scratch,
        compiler_params=pltpu.CompilerParams(collective_id=0, has_side_effects=True),
        name="step",
    )(*arrays)
    grad, gw = pl.pallas_call(
        emit,
        out_shape=(
            jax.ShapeDtypeStruct(grad.shape, BF),
            jax.ShapeDtypeStruct(gw.shape, F32),
        ),
        in_specs=[in_vmem] * 2,
        out_specs=(in_vmem,) * 2,
        name="emit",
    )(grad, gw)
    return (grad[None], gw)


def solution(mesh):
    return jax.shard_map(
        per_device,
        mesh=mesh,
        in_specs=(
            P("snap", "dom", None),
            P(),
            P(),
            P(),
            P(),
            P("snap", "dom", None),
            P("snap", "dom", None),
            P("snap", "dom", None, None),
            P(None, ("dom", "snap")),
            P(None, ("dom", "snap"), None),
        ),
        out_specs=(P("snap", "dom", None), P("snap", None)),
        check_vma=False,
    )
```

time: 83.6 us -> 67 us (0.80)
  the two profiles are of different devices: /device:TPU:32 before, /device:TPU:8 now
where the time goes in v2:
time: 67 us; the launch traced here: 66.9 us
  Pallas kernels  66.2 us (99%)
    pallas_call x1, Pallas kernels, per_device(): pl.pallas_call(functools.partial(kernel, (nz, nx, ny)), out_shape=(jax.Sh...  64.5 us
    pallas_call x1, Pallas kernels, per_device(): pl.pallas_call(emit, out_shape=(jax.ShapeDtypeStruct(grad.shape, BF), jax...  1.72 us

profile of v2, /device:TPU:8, one launch (start us, length us, event | category | flops | bytes accessed | tf_op | source)
XLA Modules:
  0.0 66.9 jit_solution(3907778258518301646)
XLA Ops:
  0.6 64.5 %step.1 = (bf16[128,512]{1,0:T(8,128)(2,1)}, f32[32,1536]{1,0:T(8,128)}) custom-call(bf16[128,512]{1,0:T(8,128)(2,1)} %bitcast.12, bf16[512,1536]{1,0:T(8,128)(2,1)} %ws_hbm.1, bf16[512,1536]{1,0:T(8,128)(2,1)} %wt_hbm.1, bf16[16,512]{1,0:T(8,128)(2,1)} %pos_hbm.1, f32[4,8]{1,0:T(4,128)} %rb_hbm.1, s32[8,128]{1,0:T(8,128)} %bitcast.13, s32[8,128]{1,0:T(8,128)} %bitcast.14, ...), custom_call_target="tpu_custom_call" | custom-call | tf_op jit(solution)/shard_map/step/pallas_call | solution.py:658
  65.2 1.7 %emit.1 = (bf16[128,512]{1,0:T(8,128)(2,1)}, f32[32,1536]{1,0:T(8,128)}) custom-call(bf16[128,512]{1,0:T(8,128)(2,1)} %get-tuple-element.6.grad_ref, f32[32,1536]{1,0:T(8,128)} %get-tuple-element.7.gw_ref), custom_call_target="tpu_custom_call" | custom-call | tf_op jit(solution)/shard_map/emit/pallas_call | solution.py:670

commit v3 on v2

--- a/solution.py
+++ b/solution.py
@@ -45,52 +45,56 @@
     )
 
 
+def ring(shift, size):
+    return min(shift, size - shift)
+
+
+def far_first(dims):
+    shifts = [()]
+    for size in dims:
+        shifts = [s + (i,) for s in shifts for i in range(abs(size))]
+    hops = lambda s: sum(ring(i, n) if n > 0 else 0.1 * i for i, n in zip(s, dims))
+    return sorted((s for s in shifts if any(s)), key=lambda s: -hops(s))
+
+
+def moved(me, shift, dims):
+    index = 0
+    for at, step, size in zip(me, shift, dims):
+        index = index * abs(size) + (lax.rem(at + step, abs(size)) if step else at)
+    return index
+
+
 class Exchange:
-    def __init__(self, count, me, device_of, src, dst, sems):
-        self.count, self.me, self.device_of = count, me, device_of
+    def __init__(self, dims, me, device_of, src, dst, sems):
+        self.dims, self.at, self.device_of = dims, me, device_of
+        self.shifts = far_first(dims)
+        self.me = moved(me, (0,) * len(dims), dims)
+        self.count = len(self.shifts) + 1
         self.src, self.dst, self.send, self.recv = src, dst, sems.at[0], sems.at[1]
 
-    def each(self, act):
-        def body(step, carry):
-            near = (step + 1) // 2
-            shift = near + (step + 1) % 2 * (self.count - 2 * near)
-            act(lax.rem(self.me + shift, self.count))
-            return carry
-
-        lax.fori_loop(1, self.count, body, 0)
-
     def start(self):
-        self.each(
-            lambda peer: copy_to(
+        for shift in self.shifts:
+            peer = moved(self.at, shift, self.dims)
+            copy_to(
                 self.src(peer),
                 self.dst.at[self.me],
-                self.send.at[peer],
-                self.recv.at[self.me],
+                self.send,
+                self.recv,
                 self.device_of(peer),
             ).start()
-        )
+
+    def all_copies(self):
+        others = self.dst.at[pl.ds(0, self.count - 1)]
+        peer = moved(self.at, self.shifts[-1], self.dims)
+        return copy_to(others, others, self.send, self.recv, self.device_of(peer))
 
     def wait_recv(self):
-        self.each(
-            lambda peer: copy_to(
-                self.src(peer),
-                self.dst.at[peer],
-                self.send.at[peer],
-                self.recv.at[peer],
-                self.device_of(peer),
-            ).wait_recv()
-        )
+        if self.count > 1:
+            self.all_copies().wait_recv()
 
     def wait_send(self):
-        self.each(
-            lambda peer: copy_to(
-                self.src(peer),
-                self.dst.at[peer],
-                self.send.at[peer],
-                self.recv.at[peer],
-                self.device_of(peer),
-            ).wait_send()
-        )
+        if self.count > 1:
+            self.all_copies().wait_send()
 
 
 def kernel(
@@ -135,10 +139,8 @@
     dt_p,
     gx_s,
     gx_r,
-    gx_v,
     xy_s,
     xy_r,
-    xz_s,
     xz_r,
     xa_r,
     zz_s,
@@ -193,7 +195,7 @@
     block = rows // n_snap
     cols = 2 * width // nx
     wrows = width // n_snap
-    xrows, zc = wrows // (nz // 2), min(4, nz)
+    zc = min(4, nz)
     zrows, zcols = wrows // (nz // zc), width // zc
     scale = (width // HEADS) ** -0.5
     scale_bf = jnp.asarray(scale, BF)
@@ -231,64 +233,40 @@
 
     barrier = pltpu.get_barrier_semaphore()
 
-    def greet_dom(step, carry):
+    for step in range(1, n_dom):
         pl.semaphore_signal(
             barrier, inc=1, device_id={"dom": lax.rem(me_d + step, n_dom)}, device_id_type=MESH
         )
-        return carry
-
-    def greet_snap(step, carry):
+    for step in range(1, n_snap):
         pl.semaphore_signal(
             barrier, inc=1, device_id={"snap": lax.rem(me_s + step, n_snap)}, device_id_type=MESH
         )
-        return carry
-
-    lax.fori_loop(1, n_dom, greet_dom, 0)
-    lax.fori_loop(1, n_snap, greet_snap, 0)
-
-    halo_x = Exchange(
-        n_dom, me_d, lambda p: {"dom": p}, lambda p: halo_s.at[p], halo_r, halo_sem
-    )
-    hid_x = Exchange(n_snap, me_s, lambda p: {"snap": p}, lambda p: hid_s.at[p], hid_r, hid_sem)
-    dh_x = Exchange(n_snap, me_s, lambda p: {"snap": p}, lambda p: dh_s.at[p], dh_r, dh_sem)
-    back_x = Exchange(
-        n_dom, me_d, lambda p: {"dom": p}, lambda p: back_s.at[p], back_r, back_sem
-    )
-    py_x = Exchange(
-        ny, me_y, lambda p: {"snap": p * 2 + me_c}, lambda p: xy_s.at[p], xy_r, xy_sem
-    )
-    pz_x = Exchange(nz, me_z, lambda p: {"dom": p * nx + me_x}, lambda p: xz_s.at[p], xz_r, xz_sem)
-    pa_x = Exchange(n_dom, me_d, lambda p: {"dom": p}, lambda p: xa_r.at[me_d], xa_r, xa_sem)
-    qz_x = Exchange(nz, me_z, lambda p: {"dom": p * nx + me_x}, lambda p: zz_s.at[p], zz_r, zz_sem)
-    qy_x = Exchange(
-        ny, me_y, lambda p: {"snap": p * 2 + me_c}, lambda p: zy_s.at[p], zy_r, zy_sem
-    )
-    qx_x = Exchange(
-        nx, me_x, lambda p: {"dom": me_z * nx + p}, lambda p: zx_r.at[me_x], zx_r, zx_sem
-    )
-    qa_x = Exchange(
-        nz, me_z, lambda p: {"dom": p * nx + me_x}, lambda p: za_r.at[me_z], za_r, za_sem
-    )
-    right, left = lax.rem(me_x + 1, nx), lax.rem(me_x + nx - 1, nx)
-    to_right, to_left = {"dom": me_z * nx + right}, {"dom": me_z * nx + left}
-    mid = width // 4
-    top, low = pl.ds(0, mid), pl.ds(mid, mid)
-
-    def neighbour(src, dst, slot, device):
-        return copy_to(src, dst, gx_sem.at[0, slot], gx_sem.at[1, slot], device)
-
-    if nx == 4:
-        across = lax.rem(me_x + 2, nx)
-        hops = [
-            neighbour(gx_s.at[across, top], gx_v.at[0], 0, to_right),
-            neighbour(gx_s.at[across, low], gx_v.at[1], 1, to_left),
-            neighbour(gx_s.at[right, low], gx_r.at[0, low], 2, to_right),
-            neighbour(gx_s.at[left, top], gx_r.at[1, top], 3, to_left),
-            neighbour(gx_v.at[2], gx_r.at[0, top], 4, to_right),
-            neighbour(gx_v.at[3], gx_r.at[1, low], 5, to_left),
-        ]
-    else:
-        hops = [neighbour(gx_s.at[right], gx_r.at[0], 0, to_right)]
+
+    dom, dom_at = (nz, nx), (me_z, me_x)
+    snap, snap_at = (ny, -2), (me_y, me_c)
+    to_dom = lambda p: {"dom": p}
+    to_snap = lambda p: {"snap": p}
+    to_x = lambda p: {"dom": me_z * nx + p}
+    to_z = lambda p: {"dom": p * nx + me_x}
+    to_y = lambda p: {"snap": p * 2 + me_c}
+    halo_x = Exchange(dom, dom_at, to_dom, lambda p: halo_s.at[p], halo_r, halo_sem)
+    hid_x = Exchange(snap, snap_at, to_snap, lambda p: hid_s.at[p], hid_r, hid_sem)
+    dh_x = Exchange(snap, snap_at, to_snap, lambda p: dh_s.at[p], dh_r, dh_sem)
+    back_x = Exchange(dom, dom_at, to_dom, lambda p: back_s.at[p], back_r, back_sem)
+    px_x = Exchange((nx,), (me_x,), to_x, lambda p: gx_s.at[p], gx_r, gx_sem)
+    py_x = Exchange((ny,), (me_y,), to_y, lambda p: xy_s.at[p], xy_r, xy_sem)
+    pz_x = Exchange((nz,), (me_z,), to_z, lambda p: xz_r.at[me_z], xz_r, xz_sem)
+    pa_x = Exchange((nx,), (me_x,), to_x, lambda p: xa_r.at[me_x], xa_r, xa_sem)
+    qz_x = Exchange((nz,), (me_z,), to_z, lambda p: zz_s.at[p], zz_r, zz_sem)
+    qy_x = Exchange((ny,), (me_y,), to_y, lambda p: zy_s.at[p], zy_r, zy_sem)
+    qx_x = Exchange((nx,), (me_x,), to_x, lambda p: zx_r.at[me_x], zx_r, zx_sem)
+    qa_x = Exchange((nz,), (me_z,), to_z, lambda p: za_r.at[me_z], za_r, za_sem)
+    pair = [
+        copy_to(zt.at[:, 1 - me_c], zt_p, pair_sem.at[0, 3], pair_sem.at[1, 3], partner)
+    ] + [
+        copy_to(dt.at[i], dt_p.at[i], pair_sem.at[0, i], pair_sem.at[1, i], partner)
+        for i in range(3)
+    ]
 
     send_f = arrive("send").astype(F32).astype(BF)
     spread = (iota((n_dom, halo), 1) // 8 == iota((n_dom, halo), 0)).astype(F32).astype(BF)
@@ -392,6 +370,7 @@
     z = z_f.astype(BF)
     tp[...] = mm(z, wt_ref[...]).astype(BF)
     zt[...] = z_f.T.astype(BF).reshape(ny, 2, width // n_snap, rows)
+    pair[0].start()
     for p in range(pairs):
         tqs[p] = stack(tp[:, 128 * p : 128 * p + 128] * scale_bf)
         t_s[p] = mm_nt(tp[:, width + 128 * p : width + 128 * p + 128], tqs[p])
@@ -404,48 +383,42 @@
         t_w[p] = w.astype(BF)
         t_b[p] = (t - w * jnp.sum(t, axis=0, keepdims=True)).astype(BF)
     for p in range(pairs):
+        dt[2, :, 128 * p : 128 * p + 128] = mm(t_w[p], cts[p]).astype(BF)
+    pair[3].start()
+    for p in range(pairs):
+        dt[1, :, 128 * p : 128 * p + 128] = mm(t_b[p], tqs[p]).astype(BF)
+    pair[2].start()
+    for p in range(pairs):
         at = 128 * p
         dq = mm_tn(t_b[p], tp[:, width + at : width + at + 128]) * scale
-        dt[:, at : at + 128] = jnp.where(half, dq[0:rows], dq[rows:]).astype(BF)
-        dt[:, width + at : width + at + 128] = mm(t_b[p], tqs[p]).astype(BF)
-        dt[:, 2 * width + at : 2 * width + at + 128] = mm(t_w[p], cts[p]).astype(BF)
-
-    pair_z = copy_to(
-        zt.at[:, 1 - me_c], zt_p, pair_sem.at[0, 0], pair_sem.at[1, 0], partner
-    )
-    pair_d = copy_to(dt, dt_p, pair_sem.at[0, 1], pair_sem.at[1, 1], partner)
-    pair_z.start()
-    pair_d.start()
-
-    d_z = ct_f + mm_nt(dt[...], wt_ref[...])
+        dt[0, :, at : at + 128] = jnp.where(half, dq[0:rows], dq[rows:]).astype(BF)
+    pair[1].start()
+
+    d_z = ct_f
+    for i in range(3):
+        d_z += mm_nt(dt[i], wt_ref[:, width * i : width * i + width])
     dh_s[...] = d_z.reshape(n_snap, block, width).astype(BF)
     dh_x.start()
     dh_r[me_s] = dh_s[me_s]
 
-    pair_z.wait_recv()
-    pair_d.wait_recv()
+    pair[0].wait_recv()
     z_both = jnp.concatenate(
         [zt[:, me_c].reshape(width // 2, rows), zt_p[...].reshape(width // 2, rows)], axis=1
     )
-    d_both = jnp.concatenate([dt[:, 0 : 2 * width], dt_p[:, 0 : 2 * width]], axis=0)
-    for i in range(nx):
-        gx_s[i] = mm(z_both, d_both[:, cols * i : cols * i + cols]).astype(BF)
-    d_both = jnp.concatenate([dt[:, 2 * width :], dt_p[:, 2 * width :]], axis=0)
-    product = mm(z_both, d_both).reshape(ny, wrows, width)
+    pair[3].wait_recv()
+    product = mm(z_both, jnp.concatenate([dt[2], dt_p[2]], axis=0)).reshape(ny, wrows, width)
     for i in range(nz):
         r, c = i // zc * zrows, i % zc * zcols
         zz_s[i] = product[:, r : r + zrows, c : c + zcols].astype(BF)
-    for hop in hops[0:4]:
-        hop.start()
     qz_x.start()
     zz_r[me_z] = zz_s[me_z]
-    if nx == 4:
-        hops[0].wait_recv()
-        hops[1].wait_recv()
-        gx_v[2] = (gx_s[right, top].astype(F32) + gx_v[0].astype(F32)).astype(BF)
-        gx_v[3] = (gx_s[left, low].astype(F32) + gx_v[1].astype(F32)).astype(BF)
-        hops[4].start()
-        hops[5].start()
+    pair[2].wait_recv()
+    pair[1].wait_recv()
+    for i in range(nx):
+        part, c = i * cols // width, i * cols % width
+        d_both = jnp.concatenate([dt[part, :, c : c + cols], dt_p[part, :, c : c + cols]], axis=0)
+        gx_s[i] = mm(z_both, d_both).astype(BF)
+    px_x.start()
 
     hid_x.wait_send()
     dh_x.wait_recv()
@@ -468,11 +441,10 @@
     back_x.start()
     back_r[me_d] = back_s[me_d]
 
-    for hop in hops[2:] if nx == 4 else hops:
-        hop.wait_recv()
-    total = gx_s[me_x].astype(F32) + gx_r[0].astype(F32)
-    if nx == 4:
-        total += gx_r[1].astype(F32)
+    px_x.wait_recv()
+    total = gx_s[me_x].astype(F32)
+    for i in range(1, nx):
+        total += gx_r[lax.rem(me_x + i, nx)].astype(F32)
     xy_s[...] = total.astype(BF).reshape(ny, wrows, cols)
     py_x.start()
     xy_r[me_y] = xy_s[me_y]
@@ -487,10 +459,9 @@
     dq = agg_t[...].T.astype(BF)
     d_own = dh_f + mm_nt(dq, ws_ref[:, :width]) + mm_nt(dkv[0:rows, :], ws_ref[:, width:])
     dh_x.wait_send()
-    pair_z.wait_send()
-    pair_d.wait_send()
-    for hop in hops:
-        hop.wait_send()
+    px_x.wait_send()
+    for copy in pair:
+        copy.wait_send()
 
     def total_of(ref, count):
         total = ref[0].astype(F32)
@@ -504,12 +475,8 @@
     zy_r[me_y] = zy_s[me_y]
 
     py_x.wait_recv()
-    total = total_of(xy_r, ny)
-    for i in range(nz):
-        r, c = i // 2 * xrows, i % 2 * 128
-        xz_s[i] = total[r : r + xrows, c : c + 128].astype(BF)
+    xz_r[me_z] = total_of(xy_r, ny).astype(BF)
     pz_x.start()
-    xz_r[me_z] = xz_s[me_z]
     qz_x.wait_send()
     py_x.wait_send()
 
@@ -525,7 +492,7 @@
     save_out.start()
 
     pz_x.wait_recv()
-    xa_r[me_d] = total_of(xz_r, nz).astype(BF)
+    xa_r[me_x] = total_of(xz_r, nz).astype(BF)
     pa_x.start()
     qx_x.wait_recv()
     za_r[me_z] = total_of(zx_r, nx).astype(BF)
@@ -538,9 +505,8 @@
         r, c = i // zc * zrows, 2 * width + i % zc * zcols
         gw_ref[r : r + zrows, c : c + zcols] = za_r[i].astype(F32)
     pa_x.wait_recv()
-    for i in range(n_dom):
-        r, c = i // nx // 2 * xrows, i % nx * cols + i // nx % 2 * 128
-        gw_ref[r : r + xrows, c : c + 128] = xa_r[i].astype(F32)
+    for i in range(nx):
+        gw_ref[:, cols * i : cols * i + cols] = xa_r[i].astype(F32)
     save_gw = pltpu.make_async_copy(gw_ref, gw_hbm, out_sem.at[1])
     save_gw.start()
     pa_x.wait_send()
@@ -549,9 +515,19 @@
     save_gw.wait()
 
 
-def emit(grad_ref, gw_ref, grad_out, gw_out):
-    grad_out[...] = grad_ref[...]
-    gw_out[...] = gw_ref[...]
+def emit(grad_in, gw_in, grad_out, gw_out, grad_v, gw_v, sem):
+    first = pltpu.make_async_copy(gw_in, gw_v, sem.at[0])
+    second = pltpu.make_async_copy(grad_in, grad_v, sem.at[1])
+    first.start()
+    second.start()
+    first.wait()
+    third = pltpu.make_async_copy(gw_v, gw_out, sem.at[2])
+    third.start()
+    second.wait()
+    fourth = pltpu.make_async_copy(grad_v, grad_out, sem.at[3])
+    fourth.start()
+    third.wait()
+    fourth.wait()
 
 
 def per_device(
@@ -567,7 +543,7 @@
     block = rows // n_snap
     cols = 2 * width // nx
     wrows = width // n_snap
-    xrows, zc = wrows // (nz // 2), min(4, nz)
+    zc = min(4, nz)
     zrows, zcols = wrows // (nz // zc), width // zc
     vm = pltpu.VMEM
     dma = pltpu.SemaphoreType.DMA
@@ -599,16 +575,14 @@
         vm((n_dom, 8, width), BF),
         vm((ny, 2, wrows, rows), BF),
         vm((ny, wrows, rows), BF),
-        vm((rows, 3 * width), BF),
-        vm((rows, 3 * width), BF),
+        vm((3, rows, width), BF),
+        vm((3, rows, width), BF),
         vm((nx, width // 2, cols), BF),
-        vm((2, width // 2, cols), BF),
-        vm((4, width // 4, cols), BF),
+        vm((nx, width // 2, cols), BF),
         vm((ny, wrows, cols), BF),
         vm((ny, wrows, cols), BF),
-        vm((nz, xrows, 128), BF),
-        vm((nz, xrows, 128), BF),
-        vm((n_dom, xrows, 128), BF),
+        vm((nz, wrows, cols), BF),
+        vm((nx, wrows, cols), BF),
         vm((nz, ny, zrows, zcols), BF),
         vm((nz, ny, zrows, zcols), BF),
         vm((ny, zrows, zcols), BF),
@@ -639,21 +613,20 @@
         vm((pairs, rows, 2 * rows), F32),
         vm((pairs, rows, 2 * rows), BF),
         vm((pairs, rows, 2 * rows), BF),
-        dma((2, n_dom)),
-        dma((2, n_snap)),
-        dma((2, n_snap)),
-        dma((2, n_dom)),
-        dma((2, 2)),
-        dma((2, 6)),
-        dma((2, ny)),
-        dma((2, nz)),
-        dma((2, n_dom)),
-        dma((2, nz)),
-        dma((2, ny)),
-        dma((2, nx)),
-        dma((2, nz)),
+        dma((2,)),
+        dma((2,)),
+        dma((2,)),
+        dma((2,)),
+        dma((2, 4)),
+        dma((2,)),
+        dma((2,)),
+        dma((2,)),
+        dma((2,)),
+        dma((2,)),
+        dma((2,)),
+        dma((2,)),
+        dma((2,)),
     ]
-    in_vmem = pl.BlockSpec(memory_space=pltpu.VMEM)
     in_any = pl.BlockSpec(memory_space=pl.ANY)
     grad, gw = pl.pallas_call(
         functools.partial(kernel, (nz, nx, ny)),
@@ -664,7 +637,9 @@
         in_specs=[in_any] * len(arrays),
         out_specs=(in_any,) * 2,
         scratch_shapes=scratch,
-        compiler_params=pltpu.CompilerParams(collective_id=0, has_side_effects=True),
+        compiler_params=pltpu.CompilerParams(
+            collective_id=0, has_side_effects=True
+        ),
         name="step",
     )(*arrays)
     grad, gw = pl.pallas_call(
@@ -673,8 +648,9 @@
             jax.ShapeDtypeStruct(grad.shape, BF),
             jax.ShapeDtypeStruct(gw.shape, F32),
         ),
-        in_specs=[in_vmem] * 2,
-        out_specs=(in_vmem,) * 2,
+        in_specs=[in_any] * 2,
+        out_specs=(in_any,) * 2,
+        scratch_shapes=[vm(grad.shape, BF), vm(gw.shape, F32), dma((4,))],
         name="emit",
     )(grad, gw)
     return (grad[None], gw)

time: 67 us -> 59.9 us (0.89)
  Pallas kernels: 66.2 us -> 59.1 us
    pallas_call x1, Pallas kernels: 64.5 us -> 57.4 us  [per_device(): pl.pallas_call(functools.partial(kernel, (nz, nx, ny)), out_shape=(jax.Sh...]
where the time goes in v3:
time: 59.9 us; the launch traced here: 59.7 us
  Pallas kernels  59.1 us (99%)
  between operations  0.64 us (1%)
    pallas_call x1, Pallas kernels, per_device(): pl.pallas_call(functools.partial(kernel, (nz, nx, ny)), out_shape=(jax.Sh...  57.4 us
    pallas_call x1, Pallas kernels, per_device(): pl.pallas_call(emit, out_shape=(jax.ShapeDtypeStruct(grad.shape, BF), jax...  1.69 us

profile of v3, /device:TPU:8, one launch (start us, length us, event | category | flops | bytes accessed | tf_op | source)
XLA Modules:
  0.0 59.7 jit_solution(4775074719233944244)
XLA Ops:
  0.6 57.4 %step.1 = (bf16[128,512]{1,0:T(8,128)(2,1)}, f32[32,1536]{1,0:T(8,128)}) custom-call(bf16[128,512]{1,0:T(8,128)(2,1)} %bitcast.12, bf16[512,1536]{1,0:T(8,128)(2,1)} %ws_hbm.1, bf16[512,1536]{1,0:T(8,128)(2,1)} %wt_hbm.1, bf16[16,512]{1,0:T(8,128)(2,1)} %pos_hbm.1, f32[4,8]{1,0:T(4,128)} %rb_hbm.1, s32[8,128]{1,0:T(8,128)} %bitcast.13, s32[8,128]{1,0:T(8,128)} %bitcast.14, ...), custom_call_target="tpu_custom_call" | custom-call | tf_op jit(solution)/shard_map/step/pallas_call | solution.py:631
  58.0 1.7 %emit.1 = (bf16[128,512]{1,0:T(8,128)(2,1)}, f32[32,1536]{1,0:T(8,128)}) custom-call(bf16[128,512]{1,0:T(8,128)(2,1)} %get-tuple-element.6.grad_in, f32[32,1536]{1,0:T(8,128)} %get-tuple-element.7.gw_in), custom_call_target="tpu_custom_call" | custom-call | tf_op jit(solution)/shard_map/emit/pallas_call | solution.py:645

commit v4 on v3

--- a/solution.py
+++ b/solution.py
@@ -233,15 +233,6 @@
 
     barrier = pltpu.get_barrier_semaphore()
 
-    for step in range(1, n_dom):
-        pl.semaphore_signal(
-            barrier, inc=1, device_id={"dom": lax.rem(me_d + step, n_dom)}, device_id_type=MESH
-        )
-    for step in range(1, n_snap):
-        pl.semaphore_signal(
-            barrier, inc=1, device_id={"snap": lax.rem(me_s + step, n_snap)}, device_id_type=MESH
-        )
-
     dom, dom_at = (nz, nx), (me_z, me_x)
     snap, snap_at = (ny, -2), (me_y, me_c)
     to_dom = lambda p: {"dom": p}
@@ -249,6 +240,13 @@
     to_x = lambda p: {"dom": me_z * nx + p}
     to_z = lambda p: {"dom": p * nx + me_x}
     to_y = lambda p: {"snap": p * 2 + me_c}
+    for shift in far_first(dom):
+        peer = to_dom(moved(dom_at, shift, dom))
+        pl.semaphore_signal(barrier, inc=1, device_id=peer, device_id_type=MESH)
+    for shift in far_first(snap):
+        peer = to_snap(moved(snap_at, shift, snap))
+        pl.semaphore_signal(barrier, inc=1, device_id=peer, device_id_type=MESH)
+
     halo_x = Exchange(dom, dom_at, to_dom, lambda p: halo_s.at[p], halo_r, halo_sem)
     hid_x = Exchange(snap, snap_at, to_snap, lambda p: hid_s.at[p], hid_r, hid_sem)
     dh_x = Exchange(snap, snap_at, to_snap, lambda p: dh_s.at[p], dh_r, dh_sem)
@@ -315,7 +313,9 @@
         total = counts[0] * eb[0:1, h : h + 1]
         for r in range(1, 4):
             total += counts[r] * eb[r : r + 1, h : h + 1]
-        cmat[h // 2, :, (h % 2) * rows : (h % 2) * rows + rows] = total
+        cmat[h // 2, :, (h % 2) * rows : (h % 2) * rows + rows] = jnp.where(
+            packed > 0, jnp.log(total), -1e30
+        )
 
     row_i = iota((rows, rows), 0)
     col_i = iota((rows, rows), 1)
@@ -344,9 +344,8 @@
     for p in range(pairs):
         attn[p] = mm_nt(ktab[:, 128 * p : 128 * p + 128], qst[p])
     for p in range(pairs):
-        c = cmat[p]
-        score = jnp.where(c > 0, attn[p], -1e30)
-        e = jnp.exp(score - jnp.max(score, axis=0, keepdims=True)) * c
+        score = attn[p] + cmat[p]
+        e = jnp.exp(score - jnp.max(score, axis=0, keepdims=True))
         w = e * (1.0 / jnp.sum(e, axis=0, keepdims=True))
         attn[p] = w
         attn_b[p] = w.astype(BF)
@@ -441,6 +440,17 @@
     back_x.start()
     back_r[me_d] = back_s[me_d]
 
+    def total_of(ref, count):
+        total = ref[0].astype(F32)
+        for i in range(1, count):
+            total += ref[i].astype(F32)
+        return total
+
+    qz_x.wait_recv()
+    zy_s[...] = total_of(zz_r, nz).astype(BF)
+    qy_x.start()
+    zy_r[me_y] = zy_s[me_y]
+
     px_x.wait_recv()
     total = gx_s[me_x].astype(F32)
     for i in range(1, nx):
@@ -463,16 +473,10 @@
     for copy in pair:
         copy.wait_send()
 
-    def total_of(ref, count):
-        total = ref[0].astype(F32)
-        for i in range(1, count):
-            total += ref[i].astype(F32)
-        return total
-
-    qz_x.wait_recv()
-    zy_s[...] = total_of(zz_r, nz).astype(BF)
-    qy_x.start()
-    zy_r[me_y] = zy_s[me_y]
+    qy_x.wait_recv()
+    zx_r[me_x] = total_of(zy_r, ny).astype(BF)
+    qx_x.start()
+    qy_x.wait_send()
 
     py_x.wait_recv()
     xz_r[me_z] = total_of(xy_r, ny).astype(BF)
@@ -480,23 +484,18 @@
     qz_x.wait_send()
     py_x.wait_send()
 
-    qy_x.wait_recv()
-    zx_r[me_x] = total_of(zy_r, ny).astype(BF)
-    qx_x.start()
-    qy_x.wait_send()
-
     back_x.wait_recv()
     came = back_r[...].astype(F32).reshape(halo, width).astype(BF)
     out_ref[...] = (d_own + mm(pick_t.astype(BF), came)).astype(BF)
     save_out = pltpu.make_async_copy(out_ref, out_hbm, out_sem.at[0])
     save_out.start()
 
+    qx_x.wait_recv()
+    za_r[me_z] = total_of(zx_r, nx).astype(BF)
+    qa_x.start()
     pz_x.wait_recv()
     xa_r[me_x] = total_of(xz_r, nz).astype(BF)
     pa_x.start()
-    qx_x.wait_recv()
-    za_r[me_z] = total_of(zx_r, nx).astype(BF)
-    qa_x.start()
     back_x.wait_send()
     pz_x.wait_send()
     qx_x.wait_send()
@@ -515,19 +514,13 @@
     save_gw.wait()
 
 
-def emit(grad_in, gw_in, grad_out, gw_out, grad_v, gw_v, sem):
-    first = pltpu.make_async_copy(gw_in, gw_v, sem.at[0])
-    second = pltpu.make_async_copy(grad_in, grad_v, sem.at[1])
+def emit(grad_in, gw_in, grad_out, gw_out, sem):
+    first = pltpu.make_async_copy(gw_in, gw_out, sem.at[0])
+    second = pltpu.make_async_copy(grad_in, grad_out, sem.at[1])
     first.start()
     second.start()
     first.wait()
-    third = pltpu.make_async_copy(gw_v, gw_out, sem.at[2])
-    third.start()
     second.wait()
-    fourth = pltpu.make_async_copy(grad_v, grad_out, sem.at[3])
-    fourth.start()
-    third.wait()
-    fourth.wait()
 
 
 def per_device(
@@ -638,10 +631,10 @@
         out_specs=(in_any,) * 2,
         scratch_shapes=scratch,
         compiler_params=pltpu.CompilerParams(
-            collective_id=0, has_side_effects=True
+            collective_id=0, has_side_effects=True, vmem_limit_bytes=48 * 2**20
         ),
         name="step",
-    )(*arrays)
+    )(*[pltpu.with_memory_space_constraint(a, pltpu.HBM) for a in arrays])
     grad, gw = pl.pallas_call(
         emit,
         out_shape=(
@@ -650,7 +643,8 @@
         ),
         in_specs=[in_any] * 2,
         out_specs=(in_any,) * 2,
-        scratch_shapes=[vm(grad.shape, BF), vm(gw.shape, F32), dma((4,))],
+        scratch_shapes=[dma((2,))],
+        compiler_params=pltpu.CompilerParams(vmem_limit_bytes=4 * 2**20),
         name="emit",
     )(grad, gw)
     return (grad[None], gw)

time: 59.9 us -> 57.7 us (0.963)
  Pallas kernels: 59.1 us -> 56.8 us
    pallas_call x1, Pallas kernels: 57.4 us -> 56.1 us  [per_device(): pl.pallas_call(functools.partial(kernel, (nz, nx, ny)), out_shape=(jax.Sh...]
    pallas_call x1, Pallas kernels: 1.69 us -> 0.74 us  [per_device(): pl.pallas_call(emit, out_shape=(jax.ShapeDtypeStruct(grad.shape, BF), jax...]
where the time goes in v4:
time: 57.7 us; the launch traced here: 57.5 us
  Pallas kernels  56.8 us (98%)
  between operations  0.64 us (1%)
    pallas_call x1, Pallas kernels, per_device(): pl.pallas_call(functools.partial(kernel, (nz, nx, ny)), out_shape=(jax.Sh...  56.1 us

profile of v4, /device:TPU:8, one launch (start us, length us, event | category | flops | bytes accessed | tf_op | source)
XLA Modules:
  0.0 57.5 jit_solution(9479501290954428907)
XLA Ops:
  0.6 56.1 %step.1 = (bf16[128,512]{1,0:T(8,128)(2,1)S(1)}, f32[32,1536]{1,0:T(8,128)S(1)}) custom-call(bf16[128,512]{1,0:T(8,128)(2,1)} %bitcast.12, bf16[512,1536]{1,0:T(8,128)(2,1)} %ws_hbm.1, bf16[512,1536]{1,0:T(8,128)(2,1)} %wt_hbm.1, bf16[16,512]{1,0:T(8,128)(2,1)} %pos_hbm.1, f32[4,8]{1,0:T(4,128)} %rb_hbm.1, s32[8,128]{1,0:T(8,128)} %bitcast.13, ...), custom_call_target="tpu_custom_call" | custom-call | tf_op jit(solution)/shard_map/step/pallas_call | solution.py:624
  56.7 0.7 %emit.1 = (bf16[128,512]{1,0:T(8,128)(2,1)}, f32[32,1536]{1,0:T(8,128)}) custom-call(bf16[128,512]{1,0:T(8,128)(2,1)S(1)} %get-tuple-element.6.grad_in, f32[32,1536]{1,0:T(8,128)S(1)} %get-tuple-element.7.gw_in), custom_call_target="tpu_custom_call" | custom-call | tf_op jit(solution)/shard_map/emit/pallas_call | solution.py:638

commit v5 on v4

--- a/solution.py
+++ b/solution.py
@@ -194,6 +194,7 @@
     table = rows + halo
     block = rows // n_snap
     cols = 2 * width // nx
+    chalf = cols // 2
     wrows = width // n_snap
     zc = min(4, nz)
     zrows, zcols = wrows // (nz // zc), width // zc
@@ -251,10 +252,16 @@
     hid_x = Exchange(snap, snap_at, to_snap, lambda p: hid_s.at[p], hid_r, hid_sem)
     dh_x = Exchange(snap, snap_at, to_snap, lambda p: dh_s.at[p], dh_r, dh_sem)
     back_x = Exchange(dom, dom_at, to_dom, lambda p: back_s.at[p], back_r, back_sem)
-    px_x = Exchange((nx,), (me_x,), to_x, lambda p: gx_s.at[p], gx_r, gx_sem)
-    py_x = Exchange((ny,), (me_y,), to_y, lambda p: xy_s.at[p], xy_r, xy_sem)
-    pz_x = Exchange((nz,), (me_z,), to_z, lambda p: xz_r.at[me_z], xz_r, xz_sem)
-    pa_x = Exchange((nx,), (me_x,), to_x, lambda p: xa_r.at[me_x], xa_r, xa_sem)
+    def halved(dims, me, device_of, src, dst, sems):
+        return [
+            Exchange(dims, me, device_of, lambda p, g=g: src(g, p), dst.at[g], sems.at[g])
+            for g in range(2)
+        ]
+
+    px_x = halved((nx,), (me_x,), to_x, lambda g, p: gx_s.at[g, p], gx_r, gx_sem)
+    py_x = halved((ny,), (me_y,), to_y, lambda g, p: xy_s.at[g, p], xy_r, xy_sem)
+    pz_x = halved((nz,), (me_z,), to_z, lambda g, p: xz_r.at[g, me_z], xz_r, xz_sem)
+    pa_x = halved((nx,), (me_x,), to_x, lambda g, p: xa_r.at[g, me_x], xa_r, xa_sem)
     qz_x = Exchange((nz,), (me_z,), to_z, lambda p: zz_s.at[p], zz_r, zz_sem)
     qy_x = Exchange((ny,), (me_y,), to_y, lambda p: zy_s.at[p], zy_r, zy_sem)
     qx_x = Exchange((nx,), (me_x,), to_x, lambda p: zx_r.at[me_x], zx_r, zx_sem)
@@ -416,8 +423,11 @@
     for i in range(nx):
         part, c = i * cols // width, i * cols % width
         d_both = jnp.concatenate([dt[part, :, c : c + cols], dt_p[part, :, c : c + cols]], axis=0)
-        gx_s[i] = mm(z_both, d_both).astype(BF)
-    px_x.start()
+        prod = mm(z_both, d_both).astype(BF)
+        gx_s[0, i] = prod[:, :chalf]
+        gx_s[1, i] = prod[:, chalf:]
+    px_x[0].start()
+    px_x[1].start()
 
     hid_x.wait_send()
     dh_x.wait_recv()
@@ -446,18 +456,26 @@
             total += ref[i].astype(F32)
         return total
 
+    px_x[0].wait_recv()
+    total = gx_s[0, me_x].astype(F32)
+    for i in range(1, nx):
+        total += gx_r[0, lax.rem(me_x + i, nx)].astype(F32)
+    xy_s[0] = total.astype(BF).reshape(ny, wrows, chalf)
+    py_x[0].start()
+    xy_r[0, me_y] = xy_s[0, me_y]
+
     qz_x.wait_recv()
     zy_s[...] = total_of(zz_r, nz).astype(BF)
     qy_x.start()
     zy_r[me_y] = zy_s[me_y]
 
-    px_x.wait_recv()
-    total = gx_s[me_x].astype(F32)
+    px_x[1].wait_recv()
+    total = gx_s[1, me_x].astype(F32)
     for i in range(1, nx):
-        total += gx_r[lax.rem(me_x + i, nx)].astype(F32)
-    xy_s[...] = total.astype(BF).reshape(ny, wrows, cols)
-    py_x.start()
-    xy_r[me_y] = xy_s[me_y]
+        total += gx_r[1, lax.rem(me_x + i, nx)].astype(F32)
+    xy_s[1] = total.astype(BF).reshape(ny, wrows, chalf)
+    py_x[1].start()
+    xy_r[1, me_y] = xy_s[1, me_y]
 
     for p in range(pairs):
         at = 128 * p
@@ -469,21 +487,22 @@
     dq = agg_t[...].T.astype(BF)
     d_own = dh_f + mm_nt(dq, ws_ref[:, :width]) + mm_nt(dkv[0:rows, :], ws_ref[:, width:])
     dh_x.wait_send()
-    px_x.wait_send()
+    px_x[0].wait_send()
+    px_x[1].wait_send()
     for copy in pair:
         copy.wait_send()
 
+    py_x[0].wait_recv()
+    xz_r[0, me_z] = total_of(xy_r.at[0], ny).astype(BF)
+    pz_x[0].start()
     qy_x.wait_recv()
     zx_r[me_x] = total_of(zy_r, ny).astype(BF)
     qx_x.start()
     qy_x.wait_send()
 
-    py_x.wait_recv()
-    xz_r[me_z] = total_of(xy_r, ny).astype(BF)
-    pz_x.start()
-    qz_x.wait_send()
-    py_x.wait_send()
-
+    py_x[1].wait_recv()
+    xz_r[1, me_z] = total_of(xy_r.at[1], ny).astype(BF)
+    pz_x[1].start()
     back_x.wait_recv()
     came = back_r[...].astype(F32).reshape(halo, width).astype(BF)
     out_ref[...] = (d_own + mm(pick_t.astype(BF), came)).astype(BF)
@@ -493,22 +512,27 @@
     qx_x.wait_recv()
     za_r[me_z] = total_of(zx_r, nx).astype(BF)
     qa_x.start()
-    pz_x.wait_recv()
-    xa_r[me_x] = total_of(xz_r, nz).astype(BF)
-    pa_x.start()
-    back_x.wait_send()
-    pz_x.wait_send()
-    qx_x.wait_send()
+    pz_x[0].wait_recv()
+    xa_r[0, me_x] = total_of(xz_r.at[0], nz).astype(BF)
+    pa_x[0].start()
+    pz_x[1].wait_recv()
+    xa_r[1, me_x] = total_of(xz_r.at[1], nz).astype(BF)
+    pa_x[1].start()
+    for exchange in (back_x, qz_x, qx_x, *py_x, *pz_x):
+        exchange.wait_send()
     qa_x.wait_recv()
     for i in range(nz):
         r, c = i // zc * zrows, 2 * width + i % zc * zcols
         gw_ref[r : r + zrows, c : c + zcols] = za_r[i].astype(F32)
-    pa_x.wait_recv()
-    for i in range(nx):
-        gw_ref[:, cols * i : cols * i + cols] = xa_r[i].astype(F32)
+    for g in range(2):
+        pa_x[g].wait_recv()
+        for i in range(nx):
+            c = cols * i + chalf * g
+            gw_ref[:, c : c + chalf] = xa_r[g, i].astype(F32)
     save_gw = pltpu.make_async_copy(gw_ref, gw_hbm, out_sem.at[1])
     save_gw.start()
-    pa_x.wait_send()
+    pa_x[0].wait_send()
+    pa_x[1].wait_send()
     qa_x.wait_send()
     save_out.wait()
     save_gw.wait()
@@ -535,6 +559,7 @@
     table = rows + halo
     block = rows // n_snap
     cols = 2 * width // nx
+    chalf = cols // 2
     wrows = width // n_snap
     zc = min(4, nz)
     zrows, zcols = wrows // (nz // zc), width // zc
@@ -570,12 +595,12 @@
         vm((ny, wrows, rows), BF),
         vm((3, rows, width), BF),
         vm((3, rows, width), BF),
-        vm((nx, width // 2, cols), BF),
-        vm((nx, width // 2, cols), BF),
-        vm((ny, wrows, cols), BF),
-        vm((ny, wrows, cols), BF),
-        vm((nz, wrows, cols), BF),
-        vm((nx, wrows, cols), BF),
+        vm((2, nx, width // 2, chalf), BF),
+        vm((2, nx, width // 2, chalf), BF),
+        vm((2, ny, wrows, chalf), BF),
+        vm((2, ny, wrows, chalf), BF),
+        vm((2, nz, wrows, chalf), BF),
+        vm((2, nx, wrows, chalf), BF),
         vm((nz, ny, zrows, zcols), BF),
         vm((nz, ny, zrows, zcols), BF),
         vm((ny, zrows, zcols), BF),
@@ -611,10 +636,10 @@
         dma((2,)),
         dma((2,)),
         dma((2, 4)),
-        dma((2,)),
-        dma((2,)),
-        dma((2,)),
-        dma((2,)),
+        dma((2, 2)),
+        dma((2, 2)),
+        dma((2, 2)),
+        dma((2, 2)),
         dma((2,)),
         dma((2,)),
         dma((2,)),

time: 57.7 us -> 55.8 us (0.967)
  Pallas kernels: 56.8 us -> 55.1 us
    pallas_call x1, Pallas kernels: 56.1 us -> 54.3 us  [per_device(): pl.pallas_call(functools.partial(kernel, (nz, nx, ny)), out_shape=(jax.Sh...]
where the time goes in v5:
time: 55.8 us; the launch traced here: 55.7 us
  Pallas kernels  55.1 us (99%)
  between operations  0.64 us (1%)
    pallas_call x1, Pallas kernels, per_device(): pl.pallas_call(functools.partial(kernel, (nz, nx, ny)), out_shape=(jax.Sh...  54.3 us

profile of v5, /device:TPU:8, one launch (start us, length us, event | category | flops | bytes accessed | tf_op | source)
XLA Modules:
  0.0 55.7 jit_solution(4894328562028358747)
XLA Ops:
  0.6 54.3 %step.1 = (bf16[128,512]{1,0:T(8,128)(2,1)S(1)}, f32[32,1536]{1,0:T(8,128)S(1)}) custom-call(bf16[128,512]{1,0:T(8,128)(2,1)} %bitcast.12, bf16[512,1536]{1,0:T(8,128)(2,1)} %ws_hbm.1, bf16[512,1536]{1,0:T(8,128)(2,1)} %wt_hbm.1, bf16[16,512]{1,0:T(8,128)(2,1)} %pos_hbm.1, f32[4,8]{1,0:T(4,128)} %rb_hbm.1, s32[8,128]{1,0:T(8,128)} %bitcast.13, ...), custom_call_target="tpu_custom_call" | custom-call | tf_op jit(solution)/shard_map/step/pallas_call | solution.py:649
  55.0 0.7 %emit.1 = (bf16[128,512]{1,0:T(8,128)(2,1)}, f32[32,1536]{1,0:T(8,128)}) custom-call(bf16[128,512]{1,0:T(8,128)(2,1)S(1)} %get-tuple-element.6.grad_in, f32[32,1536]{1,0:T(8,128)S(1)} %get-tuple-element.7.gw_in), custom_call_target="tpu_custom_call" | custom-call | tf_op jit(solution)/shard_map/emit/pallas_call | solution.py:663

commit v6 on v5

--- a/solution.py
+++ b/solution.py
@@ -109,8 +109,8 @@
     send_hbm,
     act_hbm,
     ct_hbm,
-    out_hbm,
-    gw_hbm,
+    out_ref,
+    gw_ref,
     x_ref,
     ws_ref,
     wt_ref,
@@ -122,9 +122,6 @@
     act_ref,
     ct_ref,
     in_sem,
-    out_ref,
-    gw_ref,
-    out_sem,
     halo_s,
     halo_r,
     hid_s,
@@ -169,8 +166,6 @@
     cts,
     tp,
     tqs,
-    t_s,
-    t_d,
     t_w,
     t_b,
     halo_sem,
@@ -334,6 +329,7 @@
     same = lax.rem(row_i, block) == lax.rem(col_i, block)
     earlier = jnp.where(col_i // block <= row_i // block, act_row, 0.0)
     allowed = jnp.where(row_i == col_i, 1.0, jnp.where(same, earlier, 0.0)).T
+    allowed = jnp.where(allowed > 0, 0.0, -1e30)
     allow[:, 0:rows] = allowed
     allow[:, rows:] = allowed
     step_1h = (iota((rows, n_snap), 0) // block == iota((rows, n_snap), 1)).astype(F32)
@@ -378,14 +374,13 @@
     zt[...] = z_f.T.astype(BF).reshape(ny, 2, width // n_snap, rows)
     pair[0].start()
     for p in range(pairs):
-        tqs[p] = stack(tp[:, 128 * p : 128 * p + 128] * scale_bf)
-        t_s[p] = mm_nt(tp[:, width + 128 * p : width + 128 * p + 128], tqs[p])
-        t_d[p] = mm_nt(tp[:, 2 * width + 128 * p : 2 * width + 128 * p + 128], cts[p])
-    for p in range(pairs):
-        score = jnp.where(allow[...] > 0, t_s[p], -1e30)
+        at = 128 * p
+        tqs[p] = stack(tp[:, at : at + 128] * scale_bf)
+        score = mm_nt(tp[:, width + at : width + at + 128], tqs[p]) + allow[...]
+        d_w = mm_nt(tp[:, 2 * width + at : 2 * width + at + 128], cts[p])
         e = jnp.exp(score - jnp.max(score, axis=0, keepdims=True))
         w = e * (1.0 / jnp.sum(e, axis=0, keepdims=True))
-        t = w * t_d[p]
+        t = w * d_w
         t_w[p] = w.astype(BF)
         t_b[p] = (t - w * jnp.sum(t, axis=0, keepdims=True)).astype(BF)
     for p in range(pairs):
@@ -506,8 +501,6 @@
     back_x.wait_recv()
     came = back_r[...].astype(F32).reshape(halo, width).astype(BF)
     out_ref[...] = (d_own + mm(pick_t.astype(BF), came)).astype(BF)
-    save_out = pltpu.make_async_copy(out_ref, out_hbm, out_sem.at[0])
-    save_out.start()
 
     qx_x.wait_recv()
     za_r[me_z] = total_of(zx_r, nx).astype(BF)
@@ -529,13 +522,9 @@
         for i in range(nx):
             c = cols * i + chalf * g
             gw_ref[:, c : c + chalf] = xa_r[g, i].astype(F32)
-    save_gw = pltpu.make_async_copy(gw_ref, gw_hbm, out_sem.at[1])
-    save_gw.start()
     pa_x[0].wait_send()
     pa_x[1].wait_send()
     qa_x.wait_send()
-    save_out.wait()
-    save_gw.wait()
 
 
 def emit(grad_in, gw_in, grad_out, gw_out, sem):
@@ -580,9 +569,6 @@
     pairs = HEADS // 2
     scratch = [vm(a.shape, a.dtype) for a in arrays] + [
         dma((len(arrays),)),
-        vm((rows, width), BF),
-        vm((wrows, 3 * width), F32),
-        dma((2,)),
         vm((n_dom, 8, width), BF),
         vm((n_dom, 8, width), BF),
         vm((n_snap, block, width), BF),
@@ -627,8 +613,6 @@
         vm((pairs, 2 * rows, 128), BF),
         vm((rows, 3 * width), BF),
         vm((pairs, 2 * rows, 128), BF),
-        vm((pairs, rows, 2 * rows), F32),
-        vm((pairs, rows, 2 * rows), F32),
         vm((pairs, rows, 2 * rows), BF),
         vm((pairs, rows, 2 * rows), BF),
         dma((2,)),
@@ -653,7 +637,7 @@
             jax.ShapeDtypeStruct((wrows, 3 * width), F32),
         ),
         in_specs=[in_any] * len(arrays),
-        out_specs=(in_any,) * 2,
+        out_specs=(pl.BlockSpec(memory_space=pltpu.VMEM),) * 2,
         scratch_shapes=scratch,
         compiler_params=pltpu.CompilerParams(
             collective_id=0, has_side_effects=True, vmem_limit_bytes=48 * 2**20

time: 55.8 us -> 55.6 us (level)
  no operation moved by 1% of the time
where the time goes in v6:
time: 55.6 us; the launch traced here: 55.4 us
  Pallas kernels  54.8 us (99%)
  between operations  0.64 us (1%)
    pallas_call x1, Pallas kernels, per_device(): pl.pallas_call(functools.partial(kernel, (nz, nx, ny)), out_shape=(jax.Sh...  54.1 us

profile of v6, /device:TPU:8, one launch (start us, length us, event | category | flops | bytes accessed | tf_op | source)
XLA Modules:
  0.0 55.4 jit_solution(9255220703340499332)
XLA Ops:
  0.6 54.1 %step.1 = (bf16[128,512]{1,0:T(8,128)(2,1)S(1)}, f32[32,1536]{1,0:T(8,128)S(1)}) custom-call(bf16[128,512]{1,0:T(8,128)(2,1)} %bitcast.12, bf16[512,1536]{1,0:T(8,128)(2,1)} %ws_hbm.1, bf16[512,1536]{1,0:T(8,128)(2,1)} %wt_hbm.1, bf16[16,512]{1,0:T(8,128)(2,1)} %pos_hbm.1, f32[4,8]{1,0:T(4,128)} %rb_hbm.1, s32[8,128]{1,0:T(8,128)} %bitcast.13, ...), custom_call_target="tpu_custom_call" | custom-call | tf_op jit(solution)/shard_map/step/pallas_call | solution.py:633
  54.7 0.7 %emit.1 = (bf16[128,512]{1,0:T(8,128)(2,1)}, f32[32,1536]{1,0:T(8,128)}) custom-call(bf16[128,512]{1,0:T(8,128)(2,1)S(1)} %get-tuple-element.6.grad_in, f32[32,1536]{1,0:T(8,128)S(1)} %get-tuple-element.7.gw_in), custom_call_target="tpu_custom_call" | custom-call | tf_op jit(solution)/shard_map/emit/pallas_call | solution.py:647
